TPU v7x, 512 devices: a whole 4x8x8 slice. The times are simulated.
512 devices in a mesh: member: 16 (over z, y_hi), dp: 32 (over y_lo, x, core).
Axes of the slice: x: 4, y: 8 (y_hi: 2, y_lo: 4; y = y_hi * 4 + y_lo), z: 8, core: 2. Of those that a mesh axis runs over, the one named last changes fastest.
Arguments:
- teacher_feats: bfloat16 [16, 512, 1024], P('member', 'dp'), may hold values from -8 to 8
- teacher_gain: float32 [16, 1024], P('member'), may hold values from 0.1 to 1.9
- teacher_head: bfloat16 [16, 1024, 12288], P('member', None, 'dp'), may hold values from -1 to 1
- teacher_bias: float32 [16, 12288], P('member', 'dp'), may hold values from -1 to 4
- student_feats: bfloat16 [512, 1024], P('member'), may hold values from -6 to 6
- student_gain: float32 [1024], replicated, may hold values from 0.1 to 1.9
- student_head: bfloat16 [1024, 12288], P('member', 'dp'), may hold values from -0.1875 to 0.1875
- student_bias: float32 [12288], P('dp'), may hold values from -1 to 4
Outputs:
- loss: float32 [], replicated
- head_grad: float32 [1024, 12288], P('member', 'dp')
- bias_grad: float32 [12288], P('dp')
All inputs are finite; a program needn't handle non-finite values.
Results may differ from a plain program's by a relative error of at most 0.022.
Values may be sent and summed in bfloat16 or wider, within the bound.
A program may use at most 64 MiB of HBM per device.

v0:
```python
import jax
import jax.numpy as jnp
from jax import lax
from jax.sharding import Mesh
from jax.sharding import PartitionSpec as P

MEMBER = ("member_0", "member_1")
DP = ("dp_0", "dp_1", "dp_2")
MEMBER_DP = ("member_0", "member_1", "dp_0", "dp_1", "dp_2")


def sent_to_all(shard, axis):
    devices = lax.axis_size(axis)
    return lax.all_to_all(
        jnp.broadcast_to(shard[None], (devices, *shard.shape)), axis, 0, 0, tiled=True
    )


def in_order(tiles, dim):
    dims = list(tiles.shape[1:])
    dims[dim] *= tiles.shape[0]
    return jnp.moveaxis(tiles, 0, dim).reshape(dims)


def gather_directly(shard, axis, dim):
    tiles = sent_to_all(shard, axis)
    return in_order(tiles, dim)


def gathered_once(shard, axis):
    leaves = jax.tree.leaves(shard)
    turns = sorted(range(len(leaves)), key=lambda k: -leaves[k].size)
    width = (1, *leaves[turns[0]].shape)[-1]
    lines = [
        jnp.pad(leaves[k].reshape(-1), (0, -leaves[k].size % width)).reshape(-1, width)
        for k in turns
    ]
    both, at, found = (sent_to_all(jnp.concatenate(lines), axis), 0, {})
    for k, line in zip(turns, lines):
        slab = both[:, at : at + len(line)].reshape(len(both), -1)
        found[k] = slab[:, : leaves[k].size].reshape(-1, *leaves[k].shape)
        at += len(line)
    numbers = iter(range(len(leaves)))
    return jax.tree.map(lambda _: found[next(numbers)], shard)


def joined_by_halves(pieces, combine):
    while len(jax.tree.leaves(pieces)[0]) > 1:
        pieces = jax.vmap(combine)(
            *(jax.tree.map(lambda part: part[side::2], pieces) for side in (0, 1))
        )
    return jax.tree.map(lambda part: part[0], pieces)


def joined_all(shard, axis, combine):
    pieces = gathered_once(shard, axis)
    return joined_by_halves(pieces, combine)


def cut_along(shard, dim, devices):
    dims = shard.shape
    tiles = shard.reshape(*dims[:dim], devices, dims[dim] // devices, *dims[dim + 1 :])
    return jnp.moveaxis(tiles, dim, 0)


def sent_and_summed(shard, axis, dim):
    devices = lax.axis_size(axis)
    tiles = lax.all_to_all(cut_along(shard, dim, devices), axis, 0, 0, tiled=True)
    return jnp.sum(tiles.astype(jnp.float32), axis=0)


def of_everyone(shard, axis):
    return sent_to_all(shard, axis).sum(axis=0)


def by_axis(shard, axes):
    for axis in axes:
        shard = lax.psum(shard, axis)
    return shard


def norm_rows(values, gain_row):
    values = values.astype(jnp.float32)
    center = values - jnp.mean(values, axis=-1, keepdims=True)
    spread = jnp.mean(center * center, axis=-1, keepdims=True)
    return center * lax.rsqrt(spread + 1e-06) * gain_row


def combine_scores(earlier, later):
    maxima = jnp.maximum(earlier[0], later[0])
    totals = earlier[1] * jnp.exp(earlier[0] - maxima) + later[1] * jnp.exp(later[0] - maxima)
    return (maxima, totals)


def row_folder(source, portion):
    return jnp.dot(source, portion, preferred_element_type=jnp.float32)


def on_device(
    teacher_feats,
    teacher_gain,
    teacher_head,
    teacher_bias,
    student_feats,
    student_gain,
    student_head,
    student_bias,
):
    members = lax.axis_size(MEMBER)
    dp_count = lax.axis_size(DP)
    normed = norm_rows(teacher_feats[0], teacher_gain[0]).astype(jnp.bfloat16)
    weights = teacher_head[0]
    offsets = teacher_bias[0]
    logits = (
        jnp.dot(gather_directly(normed, DP, 0), weights, preferred_element_type=jnp.float32)
        + offsets
    )
    images = logits.shape[0]
    local_max = jnp.max(logits, axis=1)
    local_total = jnp.sum(jnp.exp(logits - local_max[:, None]), axis=1)
    maxima, totals = joined_all((local_max, local_total), DP, combine_scores)
    log_norm = maxima + jnp.log(totals)
    log_prob = logits - log_norm[:, None]
    normed_s = norm_rows(student_feats, student_gain).astype(jnp.bfloat16)
    col_count = student_head.shape[1]
    classes = col_count * dp_count
    summed = sent_and_summed(log_prob.astype(jnp.bfloat16), MEMBER, 0)
    target = summed / members
    student_logits = row_folder(normed_s, gather_directly(student_head, MEMBER, 0))
    alphas = jnp.exp(student_logits + student_bias)
    alpha_sum = of_everyone(jnp.sum(alphas, axis=1), DP)
    partial_value = jnp.sum(-lax.lgamma(alpha_sum) / dp_count) + jnp.sum(
        lax.lgamma(alphas) - (alphas - 1.0) * target
    )
    term_signal = alphas * (lax.digamma(alphas) - lax.digamma(alpha_sum)[:, None] - target)
    loss_value = by_axis(partial_value, MEMBER_DP) / (images * classes)
    columns = normed_s.astype(jnp.float32)
    head_grad = (
        sent_and_summed(
            lax.dot_general(
                columns,
                term_signal,
                (((0,), (0,)), ((), ())),
                precision=lax.Precision.HIGHEST,
                preferred_element_type=jnp.float32,
            ).astype(jnp.bfloat16),
            MEMBER,
            0,
        )
        / images
    )
    bias_grad = of_everyone(jnp.sum(term_signal, axis=0), MEMBER) / images
    return (loss_value, head_grad, bias_grad)


def solution(mesh):
    torus = Mesh(
        mesh.devices.reshape(8, 2, 4, 4, 2), ("member_0", "member_1", "dp_0", "dp_1", "dp_2")
    )
    placed = (
        P(MEMBER, DP, None),
        P(MEMBER, None),
        P(MEMBER, None, DP),
        P(MEMBER, DP),
        P(MEMBER, None),
        P(),
        P(MEMBER, DP),
        P(DP),
    )
    return jax.shard_map(
        on_device,
        mesh=torus,
        in_specs=placed,
        out_specs=(P(), P(MEMBER, DP), P(DP)),
        check_vma=False,
    )
```

profile of v0, /device:TPU:1, one launch (start us, length us, event | category | flops | bytes accessed | tf_op | source)
XLA Modules:
  0.0 218.6 jit_solution(2406226476668857303)
XLA Ops:
  0.6 0.9 convert_reduce_fusion.3
  1.6 0.9 fusion.12
  2.6 0.8 fusion.22
  3.4 1.1 broadcast_in_dim.15
  4.5 10.6 %all-to-all-start.2 = ((bf16[32,16,1024]{2,1,0:T(8,128)(2,1)}), bf16[32,16,1024]{2,1,0:T(8,128)(2,1)S(1)}, u32[]{:S(2)}, u32[]{:S(2)}) async-start(bf16[32,16,1024]{2,1,0:T(8,128)(2,1)} %broadcast_in_dim.15), calls=%async_computation.2 | async-start | bytes 2097152 | tf_op jit(solution)/shard_map/all_to_all | solution.py:14
  15.1 26.7 %all-to-all-done.2 = bf16[32,16,1024]{2,1,0:T(8,128)(2,1)S(1)} async-done(((bf16[32,16,1024]{2,1,0:T(8,128)(2,1)}), bf16[32,16,1024]{2,1,0:T(8,128)(2,1)S(1)}, u32[]{:S(2)}, u32[]{:S(2)}) %all-to-all-start.2) | async-done | bytes 1048608 | tf_op jit(solution)/shard_map/all_to_all | solution.py:14
  41.9 0.8 fusion.36
  43.0 13.3 %all_to_all.37 = f32[32,2,512]{2,1,0:T(2,128)S(1)} all-to-all(f32[32,2,512]{2,1,0:T(2,128)S(1)} %broadcast_in_dim.16), channel_id=1, replica_groups=mesh['member_0'=8,'member_1'=2,'dp_0'=4,'dp_1'=4,'dp_2'=2] {'dp_0','dp_1..., dimensions={0} | all-to-all | bytes 262144 | tf_op jit(solution)/shard_map/all_to_all | solution.py:14
  57.1 24.4 %all_to_all.38 = bf16[16,32,384]{2,1,0:T(8,128)(2,1)S(1)} all-to-all(bf16[16,32,384]{2,1,0:T(8,128)(2,1)S(1)} %bitcast.31), channel_id=1, replica_groups=mesh['member_0'=8,'member_1'=2,'dp_0'=4,'dp_1'=4,'dp_2'=2] {'member_0','..., dimensions={0} | all-to-all | bytes 786432 | tf_op jit(solution)/shard_map/all_to_all | solution.py:68
  81.5 1.0 broadcast_in_dim.12
  82.5 8.3 %all-to-all-start = ((bf16[16,64,384]{2,1,0:T(8,128)(2,1)}), bf16[16,64,384]{2,1,0:T(8,128)(2,1)S(1)}, u32[]{:S(2)}, u32[]{:S(2)}) async-start(bf16[16,64,384]{2,1,0:T(8,128)(2,1)} %broadcast_in_dim.12), calls=%async_computation | async-start | bytes 1572864 | tf_op jit(solution)/shard_map/all_to_all | solution.py:14
  91.2 17.5 %all-to-all-done = bf16[16,64,384]{2,1,0:T(8,128)(2,1)S(1)} async-done(((bf16[16,64,384]{2,1,0:T(8,128)(2,1)}), bf16[16,64,384]{2,1,0:T(8,128)(2,1)S(1)}, u32[]{:S(2)}, u32[]{:S(2)}) %all-to-all-start) | async-done | bytes 786464 | tf_op jit(solution)/shard_map/all_to_all | solution.py:14
  108.7 1.2 subtract_reduce_fusion
  109.9 20.9 %all_to_all.39 = f32[32,1,32]{2,1,0:T(1,128)S(1)} all-to-all(f32[32,1,32]{2,1,0:T(1,128)S(1)} %broadcast_in_dim.13), channel_id=1, replica_groups=mesh['member_0'=8,'member_1'=2,'dp_0'=4,'dp_1'=4,'dp_2'=2] {'dp_0','dp_1..., dimensions={0} | all-to-all | bytes 8192 | tf_op jit(solution)/shard_map/all_to_all | solution.py:14
  131.8 6.1 %all-to-all-start.6 = ((f32[16,1,384]{2,1,0:T(1,128)}), f32[16,1,384]{2,1,0:T(1,128)S(1)}, u32[]{:S(2)}, u32[]{:S(2)}) async-start(f32[16,1,384]{2,1,0:T(1,128)} %broadcast_in_dim.17), calls=%async_computation.6 | async-start | bytes 49152 | tf_op jit(solution)/shard_map/all_to_all | solution.py:14
  137.9 1.8 convolution_convert_fusion
  139.7 9.6 %all-to-all-done.6 = f32[16,1,384]{2,1,0:T(1,128)S(1)} async-done(((f32[16,1,384]{2,1,0:T(1,128)}), f32[16,1,384]{2,1,0:T(1,128)S(1)}, u32[]{:S(2)}, u32[]{:S(2)}) %all-to-all-start.6) | async-done | bytes 24608 | tf_op jit(solution)/shard_map/all_to_all | solution.py:14
  149.3 3.6 %all-to-all-start.5 = ((bf16[16,64,384]{2,1,0:T(8,128)(2,1)}), bf16[16,64,384]{2,1,0:T(8,128)(2,1)S(1)}, u32[]{:S(2)}, u32[]{:S(2)}) async-start(bf16[16,64,384]{2,1,0:T(8,128)(2,1)} %bitcast.12), calls=%async_computation.5 | async-start | bytes 1572864 | tf_op jit(solution)/shard_map/all_to_all | solution.py:68
  152.9 0.7 multiply_reduce_fusion
  154.9 22.8 %psum.35 = f32[]{:T(128)} all-reduce(f32[]{:T(128)S(6)} %add.96), channel_id=1, replica_groups=mesh['member_0'=8,'member_1'=2,'dp_0'=4,'dp_1'=4,'dp_2'=2] {'member_0'}, use_global_device_ids=true, to_apply=%region_11.12 | all-reduce | flops 1 | bytes 8 | tf_op jit(solution)/shard_map/psum | solution.py:78
  177.7 10.6 %psum.36 = f32[]{:T(128)} all-reduce(f32[]{:T(128)} %psum.35), channel_id=1, replica_groups=mesh['member_0'=8,'member_1'=2,'dp_0'=4,'dp_1'=4,'dp_2'=2] {'member_1'}, use_global_device_ids=true, to_apply=%region_12.13 | all-reduce | flops 1 | bytes 8 | tf_op jit(solution)/shard_map/psum | solution.py:78
  188.3 7.6 %psum.37 = f32[]{:T(128)} all-reduce(f32[]{:T(128)} %psum.36), channel_id=1, replica_groups=mesh['member_0'=8,'member_1'=2,'dp_0'=4,'dp_1'=4,'dp_2'=2] {'dp_0'}, use_global_device_ids=true, to_apply=%region_13.14 | all-reduce | flops 1 | bytes 8 | tf_op jit(solution)/shard_map/psum | solution.py:78
  195.9 7.5 %psum.38 = f32[]{:T(128)} all-reduce(f32[]{:T(128)} %psum.37), channel_id=1, replica_groups=mesh['member_0'=8,'member_1'=2,'dp_0'=4,'dp_1'=4,'dp_2'=2] {'dp_1'}, use_global_device_ids=true, to_apply=%region_14.15 | all-reduce | flops 1 | bytes 8 | tf_op jit(solution)/shard_map/psum | solution.py:78
  203.4 12.0 %psum.39 = f32[]{:T(128)} all-reduce(f32[]{:T(128)} %psum.38), channel_id=1, replica_groups=mesh['member_0'=8,'member_1'=2,'dp_0'=4,'dp_1'=4,'dp_2'=2] {'dp_2'}, use_global_device_ids=true, to_apply=%region_15.16 | all-reduce | flops 1 | bytes 8 | tf_op jit(solution)/shard_map/psum | solution.py:78
  (57 shorter events, 3.9 us)
Async XLA Ops:
  0.6 41.2 %copy-start = (bf16[1,1024,384]{2,1,0:T(8,128)(2,1)S(1)}, bf16[1,1024,384]{2,1,0:T(8,128)(2,1)}, u32[]{:S(2)}) copy-start(bf16[1,1024,384]{2,1,0:T(8,128)(2,1)} %param.10) | copy-start | bytes 2359300
  4.5 10.6 %copy-start.4 = (f32[1,384]{1,0:T(1,128)S(1)}, f32[1,384]{1,0:T(1,128)}, u32[]{:S(2)}) copy-start(f32[1,384]{1,0:T(1,128)} %param.11) | copy-start | bytes 4612
  4.5 37.3 %all-to-all-start.2 = ((bf16[32,16,1024]{2,1,0:T(8,128)(2,1)}), bf16[32,16,1024]{2,1,0:T(8,128)(2,1)S(1)}, u32[]{:S(2)}, u32[]{:S(2)}) async-start(bf16[32,16,1024]{2,1,0:T(8,128)(2,1)} %broadcast_in_dim.15), calls=%async_computation.2 | async-start | bytes 2097152 | tf_op jit(solution)/shard_map/all_to_all | solution.py:14
  56.7 24.7 %copy-start.2 = (bf16[64,384]{1,0:T(8,128)(2,1)S(1)}, bf16[64,384]{1,0:T(8,128)(2,1)}, u32[]{:S(2)}) copy-start(bf16[64,384]{1,0:T(8,128)(2,1)} %param.14) | copy-start | bytes 147460
  81.5 9.3 %copy-start.1 = (bf16[32,1024]{1,0:T(8,128)(2,1)S(1)}, bf16[32,1024]{1,0:T(8,128)(2,1)}, u32[]{:S(2)}) copy-start(bf16[32,1024]{1,0:T(8,128)(2,1)} %param.12) | copy-start | bytes 196612
  82.4 26.2 %copy-start.3 = (f32[1024]{0:T(1024)S(1)}, f32[1024]{0:T(1024)}, u32[]{:S(2)}) copy-start(f32[1024]{0:T(1024)} %param.13) | copy-start | bytes 12292
  82.5 26.2 %copy-start.5 = (f32[384]{0:T(512)S(1)}, f32[384]{0:T(512)}, u32[]{:S(2)}) copy-start(f32[384]{0:T(512)} %param.15) | copy-start | bytes 4612
  82.5 26.2 %all-to-all-start = ((bf16[16,64,384]{2,1,0:T(8,128)(2,1)}), bf16[16,64,384]{2,1,0:T(8,128)(2,1)S(1)}, u32[]{:S(2)}, u32[]{:S(2)}) async-start(bf16[16,64,384]{2,1,0:T(8,128)(2,1)} %broadcast_in_dim.12), calls=%async_computation | async-start | bytes 1572864 | tf_op jit(solution)/shard_map/all_to_all | solution.py:14
  131.8 17.5 %all-to-all-start.6 = ((f32[16,1,384]{2,1,0:T(1,128)}), f32[16,1,384]{2,1,0:T(1,128)S(1)}, u32[]{:S(2)}, u32[]{:S(2)}) async-start(f32[16,1,384]{2,1,0:T(1,128)} %broadcast_in_dim.17), calls=%async_computation.6 | async-start | bytes 49152 | tf_op jit(solution)/shard_map/all_to_all | solution.py:14
  149.3 67.4 %all-to-all-start.5 = ((bf16[16,64,384]{2,1,0:T(8,128)(2,1)}), bf16[16,64,384]{2,1,0:T(8,128)(2,1)S(1)}, u32[]{:S(2)}, u32[]{:S(2)}) async-start(bf16[16,64,384]{2,1,0:T(8,128)(2,1)} %bitcast.12), calls=%async_computation.5 | async-start | bytes 1572864 | tf_op jit(solution)/shard_map/all_to_all | solution.py:68
where the time goes:
time: 219 us
  blocking collectives  119 us (54%)
  waiting for transfers between devices  53.8 us (25%)
  starting transfers between devices  28.6 us (13%)
  other arithmetic  6.17 us (3%)
  between operations  3.89 us (2%)
  matrix products  3.74 us (2%)
  local copies, waits for them, and re-layouts  3.24 us (1%)
    psum x5, blocking collectives, by_axis(): shard = lax.psum(shard, axis)  60.6 us
    all_to_all x3, waiting for transfers between devices, sent_to_all(): lax.all_to_all(jnp.broadcast_to(shard[None], (devices, *shard.shape)), ax...  53.8 us
    all_to_all x2, blocking collectives, sent_to_all(): lax.all_to_all(jnp.broadcast_to(shard[None], (devices, *shard.shape)), ax...  34.2 us
    all_to_all x3, starting transfers between devices, sent_to_all(): lax.all_to_all(jnp.broadcast_to(shard[None], (devices, *shard.shape)), ax...  25 us
    all_to_all x1, blocking collectives, sent_and_summed(): lax.all_to_all(cut_along(shard, dim, devices), axis, 0, 0, tiled=True)  24.4 us
  transfers between devices with their start and end apart: 4, of which 3 were waited for; matrix products, arithmetic and copies ran while one was open for 2% of the time, Pallas kernels for 0%

commit v1 on v0

v1 whole, which is shorter than its diff:
```python
import functools

import jax
import jax.numpy as jnp
from jax import lax
from jax.experimental import pallas as pl
from jax.experimental.pallas import tpu as pltpu
from jax.sharding import Mesh
from jax.sharding import PartitionSpec as P

MEMBER = ("member_0", "member_1")
DP = ("dp_0", "dp_1", "dp_2")
AXES = MEMBER + DP
LANES = 128
F32 = jnp.float32
BF16 = jnp.bfloat16
NT = (((1,), (1,)), ((), ()))


def norm_rows(values, gain_row):
    values = values.astype(F32)
    center = values - jnp.mean(values, axis=-1, keepdims=True)
    spread = jnp.mean(center * center, axis=-1, keepdims=True)
    return center * lax.rsqrt(spread + 1e-06) * gain_row


def gamma_parts(x):
    small = x < 8.0
    base = jnp.where(small, x, 1.0)
    product = base
    harmonic = 1.0 / base
    for step in range(1, 8):
        product = product * (base + step)
        harmonic = harmonic + 1.0 / (base + step)
    big = jnp.where(small, x + 8.0, x)
    log_big = jnp.log(big)
    inv = 1.0 / big
    inv2 = inv * inv
    lgamma = (big - 0.5) * log_big - big + 0.9189385332046727
    lgamma = lgamma + inv * (1.0 / 12 - inv2 * (1.0 / 360 - inv2 * (1.0 / 1260)))
    digamma = log_big - 0.5 * inv - inv2 * (1.0 / 12 - inv2 * (1.0 / 120 - inv2 * (1.0 / 252)))
    lgamma = lgamma - jnp.where(small, jnp.log(product), 0.0)
    digamma = digamma - jnp.where(small, harmonic, 0.0)
    return lgamma, digamma


def start_copy(src, dst, send_sem, recv_sem, device):
    pltpu.make_async_remote_copy(
        src_ref=src,
        dst_ref=dst,
        send_sem=send_sem,
        recv_sem=recv_sem,
        device_id=device,
        device_id_type=pl.DeviceIdType.MESH,
    ).start()


def wait_bytes(ref, sem):
    pltpu.make_async_copy(ref, ref, sem).wait()


def step_kernel(
    sizes,
    tf_h, tg_h, w_h, tb_h, sf_h, sg_h, sh_h, sb_h,
    hg_o, bias_o, loss_o,
    tfv, tgv, wv, tbv, sfv, sgv, sbv,
    xn, wt, tbt, lg, send, rb, tz, tb_s, tp,
    bm, bs, st, vs, vr, vz, vp,
    sn, shb, sws, swr, sbt, ad, asum, az, al_s,
    bc, bg_s, bgr, bh, bp, hs, hr, ht, hb, hp,
    ld, l_s, lz, lh, lp,
    in_sems, xn_sems, sn_sems, rb_sems, one, out,
):
    Z, H, Y, X, C = sizes
    z, h, y, x, c = (lax.axis_index(a) for a in AXES)
    dpn = Y * X * C
    me = (y * X + x) * C + c
    D = xn.shape[2]
    rows_t = xn.shape[1]
    L = wt.shape[0]
    cb = L // Z
    half_blocks = dpn // H
    ih = half_blocks * rows_t
    rows_s = ih // Z
    q = rows_s // rows_t
    images = ih * H

    def at(nz=None, nh=None, ny=None, nx=None, nc=None):
        new = (nz, nh, ny, nx, nc)
        return tuple(old if n is None else n for old, n in zip((z, h, y, x, c), new))

    def spot(py, px, pc):
        d = (py * X + px) * C + pc
        m = d // q
        return (m % H) * half_blocks + (m // H) * q + d % q

    def ring(k):
        return lax.rem(z + k, Z)

    z_order = sorted(range(1, Z), key=lambda k: -min(k, Z - k))
    plane = [
        (lax.rem(y + i, Y), lax.rem(x + j, X), lax.rem(c + k, C))
        for i in reversed(range(Y))
        for j in range(X)
        for k in range(C)
        if i or j or k
    ]

    loads = [
        pltpu.make_async_copy(src, dst, in_sems.at[i])
        for i, (src, dst) in enumerate(
            [
                (tf_h.at[0], tfv),
                (tg_h, tgv),
                (sf_h, sfv),
                (sg_h, sgv),
                (sh_h, shb.at[h]),
                (tb_h, tbv),
                (sb_h, sbv),
                (w_h.at[0], wv),
            ]
        )
    ]
    for load in loads:
        load.start()
    barrier = pltpu.get_barrier_semaphore()
    peers = [at(ny=a, nx=b, nc=e) for a, b, e in plane]
    peers += [at(nz=ring(k)) for k in range(1, Z)] + [at(nh=1 - h)]
    for peer in peers:
        pl.semaphore_signal(barrier, 1, device_id=peer, device_id_type=pl.DeviceIdType.MESH)

    own = spot(y, x, c)
    loads[0].wait()
    loads[1].wait()
    xn[own] = norm_rows(tfv[...], tgv[...]).astype(BF16)
    loads[2].wait()
    loads[3].wait()
    sn[pl.ds(z * C, C)] = norm_rows(sfv[...], sgv[...]).astype(BF16).reshape(C, rows_s // C, D)
    loads[4].wait()
    pl.semaphore_wait(barrier, len(peers))

    def forward(block, device):
        start_copy(xn.at[block], xn.at[block], out.at[0], xn_sems.at[block], device)

    for k in reversed(range(1, Y)):
        forward(own, at(ny=lax.rem(y + k, Y)))
    for j in range(1, X):
        forward(own, at(nx=lax.rem(x + j, X)))
    for e in range(1, C):
        forward(own, at(nc=lax.rem(c + e, C)))
    start_copy(shb.at[h], shb.at[h], out.at[1], one.at[0], at(nh=1 - h))
    mine = z * C + c
    for k in z_order:
        start_copy(sn.at[mine], sn.at[mine], out.at[2], sn_sems.at[mine], at(nz=ring(k)))

    loads[5].wait()
    loads[6].wait()
    tbt[...] = jnp.broadcast_to(tbv[...], (LANES, L)).T
    sbt[...] = jnp.broadcast_to(sbv[...], (LANES, L)).T
    loads[7].wait()
    for k in range(D // LANES):
        part = slice(k * LANES, (k + 1) * LANES)
        wt[:, part] = wv[part, :].astype(F32).T.astype(BF16)

    for k in range(1, Y):
        py = lax.rem(y + k, Y)
        block = spot(py, x, c)
        wait_bytes(xn.at[block], xn_sems.at[block])
        for j in range(1, X):
            forward(block, at(nx=lax.rem(x + j, X)))
        for e in range(1, C):
            forward(block, at(nc=lax.rem(c + e, C)))

    wait_bytes(shb.at[1 - h], one.at[0])
    turned = shb[...].astype(F32).reshape(shb.shape[0] * shb.shape[1], L).T
    sws[...] = turned.astype(BF16).reshape(Z, cb, LANES)
    for k in z_order:
        start_copy(sws.at[ring(k)], swr.at[z], out.at[3], one.at[1], at(nz=ring(k)))
    swr[z] = sws[z]

    for j in range(1, X):
        px = lax.rem(x + j, X)
        for k in range(Y):
            block = spot(lax.rem(y + k, Y), px, c)
            wait_bytes(xn.at[block], xn_sems.at[block])
            for e in range(1, C):
                forward(block, at(nc=lax.rem(c + e, C)))
    for k in range(1, Z):
        block = ring(k) * C + c
        wait_bytes(sn.at[block], sn_sems.at[block])
        for e in range(1, C):
            start_copy(
                sn.at[block], sn.at[block], out.at[2], sn_sems.at[block], at(nc=lax.rem(c + e, C))
            )
    for e in range(1, C):
        pc = lax.rem(c + e, C)
        for k in range(Y):
            for j in range(X):
                block = spot(lax.rem(y + k, Y), lax.rem(x + j, X), pc)
                wait_bytes(xn.at[block], xn_sems.at[block])

    for a in range(H):
        held = xn[a * half_blocks : (a + 1) * half_blocks].reshape(ih, D)
        lg[a] = lax.dot_general(wt[...], held, NT, preferred_element_type=F32)
    for k in z_order + [0]:
        to = ring(k)
        rows = pl.ds(pl.multiple_of(to * cb, 16), cb)
        part = lg[:, rows, :] + tbt[rows, 0:1][None]
        top = jnp.max(part, axis=1, keepdims=True)
        part = part - top
        send[to] = part.astype(BF16)
        bm[to] = top
        bs[to] = jnp.sum(jnp.exp(part), axis=1, keepdims=True)
        if k:
            start_copy(send.at[to], rb.at[z], out.at[4], rb_sems.at[z], at(nz=to))
    tops = bm[...]
    top = jnp.max(tops, axis=0)
    st[me] = top + jnp.log(jnp.sum(bs[...] * jnp.exp(tops - top[None]), axis=0))
    for a, b, e in plane:
        start_copy(st.at[me], st.at[me], out.at[5], one.at[2], at(ny=a, nx=b, nc=e))

    for e in range(1, C):
        pc = lax.rem(c + e, C)
        for k in range(1, Z):
            block = ring(k) * C + pc
            wait_bytes(sn.at[block], sn_sems.at[block])
    wait_bytes(swr.at[pl.ds(0, Z - 1)], one.at[1])
    scores = jnp.zeros((cb, ih), F32)
    for k in range(Z):
        part = slice(k * LANES, (k + 1) * LANES)
        scores = scores + lax.dot_general(
            swr[k], sn[:, :, part].reshape(ih, LANES), NT, preferred_element_type=F32
        )
    my_rows = pl.ds(pl.multiple_of(z * cb, 16), cb)
    alphas = jnp.exp(scores + sbt[my_rows, 0:1])
    al_s[...] = alphas
    ad[me] = jnp.sum(alphas, axis=0, keepdims=True)
    for a, b, e in plane:
        start_copy(ad.at[me], ad.at[me], out.at[6], one.at[3], at(ny=a, nx=b, nc=e))

    wait_bytes(st.at[pl.ds(0, dpn - 1)], one.at[2])
    tops = st[...]
    top = jnp.max(tops, axis=0)
    log_norm = top + jnp.log(jnp.sum(jnp.exp(tops - top[None]), axis=0))
    vs[...] = bm[...] - log_norm[None]
    for k in z_order:
        start_copy(vs.at[ring(k)], vr.at[z], out.at[7], one.at[4], at(nz=ring(k)))
    vr[z] = vs[z]

    wait_bytes(ad.at[pl.ds(0, dpn - 1)], one.at[3])
    asum[...] = jnp.sum(ad[...], axis=0)
    for k in z_order:
        start_copy(asum, az.at[z], out.at[8], one.at[5], at(nz=ring(k)))
    az[z] = asum[...]
    lgamma, digamma = gamma_parts(al_s[...])

    total = send[z].astype(F32)
    for k in range(1, Z):
        wait_bytes(rb.at[ring(k)], rb_sems.at[ring(k)])
        total = total + rb[ring(k)].astype(F32)
    tz[...] = total
    tb_s[...] = tz[1 - h].astype(BF16)
    start_copy(tb_s, tp, out.at[9], one.at[6], at(nh=1 - h))
    wait_bytes(vr.at[pl.ds(0, Z - 1)], one.at[4])
    vz[...] = jnp.sum(vr[...], axis=0)
    start_copy(vz.at[1 - h], vp, out.at[10], one.at[7], at(nh=1 - h))
    wait_bytes(az.at[pl.ds(0, Z - 1)], one.at[5])
    lgamma_sum, digamma_sum = gamma_parts(jnp.sum(az[...], axis=0))
    wait_bytes(vp, one.at[7])
    shift = vz[h] + vp[...]
    wait_bytes(tp, one.at[6])
    target = (tz[h] + tp[...].astype(F32) + shift) / (Z * H)

    alphas = al_s[...]
    signal = alphas * (digamma - digamma_sum - target)
    terms = jnp.sum(lgamma - (alphas - 1.0) * target, axis=0, keepdims=True)
    terms = terms - lgamma_sum / (Z * dpn)
    ld[me] = jnp.broadcast_to(jnp.sum(terms, axis=1, keepdims=True), (1, LANES))
    for a, b, e in plane:
        start_copy(ld.at[me], ld.at[me], out.at[11], one.at[8], at(ny=a, nx=b, nc=e))

    high = signal.astype(BF16)
    rest = signal - high.astype(F32)
    mid = rest.astype(BF16)
    low = (rest - mid.astype(F32)).astype(BF16)
    parts = lax.dot_general(
        jnp.concatenate([high, mid, low], axis=0),
        sn[...].reshape(ih, D),
        (((1,), (0,)), ((), ())),
        preferred_element_type=F32,
    )
    grad = parts[:cb] + parts[cb : 2 * cb] + parts[2 * cb :]
    for k in range(Z):
        hs[k] = grad[:, k * LANES : (k + 1) * LANES].astype(BF16)
    for k in z_order:
        start_copy(hs.at[ring(k)], hr.at[z], out.at[12], one.at[9], at(nz=ring(k)))
    hr[z] = hs[z]
    bc[...] = jnp.zeros_like(bc)
    bc[my_rows, :] = jnp.broadcast_to(jnp.sum(signal, axis=1, keepdims=True), (cb, LANES))
    bg_s[...] = bc[...].T[0:1]
    for k in z_order:
        start_copy(bg_s, bgr.at[z], out.at[13], one.at[10], at(nz=ring(k)))
    bgr[z] = bg_s[...]

    wait_bytes(ld.at[pl.ds(0, dpn - 1)], one.at[8])
    l_s[...] = jnp.sum(ld[...], axis=0)
    for k in z_order:
        start_copy(l_s, lz.at[z], out.at[14], one.at[11], at(nz=ring(k)))
    lz[z] = l_s[...]

    wait_bytes(hr.at[pl.ds(0, Z - 1)], one.at[9])
    rows = hr[...].astype(F32).reshape(L, LANES).T
    ht[...] = rows.reshape(H, LANES // H, L)
    hb[...] = ht[1 - h].astype(BF16)
    start_copy(hb, hp, out.at[15], one.at[12], at(nh=1 - h))
    wait_bytes(bgr.at[pl.ds(0, Z - 1)], one.at[10])
    bh[...] = jnp.sum(bgr[...], axis=0)
    start_copy(bh, bp, out.at[16], one.at[13], at(nh=1 - h))
    wait_bytes(lz.at[pl.ds(0, Z - 1)], one.at[11])
    lh[...] = jnp.sum(lz[...], axis=0)
    start_copy(lh, lp, out.at[17], one.at[14], at(nh=1 - h))

    wait_bytes(bp, one.at[13])
    bias_o[...] = (bh[...] + bp[...]) / images
    wait_bytes(lp, one.at[14])
    loss_o[...] = (lh[...] + lp[...]) / (images * (L * dpn))
    wait_bytes(hp, one.at[12])
    hg_o[...] = (ht[h] + hp[...].astype(F32)) / images

    sent = [
        xn.at[pl.ds(0, dpn - 1)],
        shb.at[h],
        sn.at[pl.ds(0, (Z - 1) * C)],
        sws.at[pl.ds(0, Z - 1)],
        send.at[pl.ds(0, Z - 1)],
        st.at[pl.ds(0, dpn - 1)],
        ad.at[pl.ds(0, dpn - 1)],
        vs.at[pl.ds(0, Z - 1)],
        az.at[pl.ds(0, Z - 1)],
        tb_s,
        vp,
        ld.at[pl.ds(0, dpn - 1)],
        hs.at[pl.ds(0, Z - 1)],
        bgr.at[pl.ds(0, Z - 1)],
        lz.at[pl.ds(0, Z - 1)],
        hb,
        bh,
        lh,
    ]
    for i, ref in enumerate(sent):
        wait_bytes(ref, out.at[i])


def on_device(sizes, tf, tg, w, tb, sf, sg, sh, sb):
    Z, H, Y, X, C = sizes
    dpn = Y * X * C
    rows_t, D = tf.shape[1:]
    L = w.shape[2]
    cb = L // Z
    ih = rows_t * dpn // H
    rows_s = sf.shape[0]
    assert D == Z * LANES and rows_s * Z == ih and sh.shape[0] * H == LANES

    def v(shape, dtype=F32):
        return pltpu.VMEM(shape, dtype)

    scratch = [
        v((rows_t, D), BF16), v((1, D)), v((D, L), BF16), v((1, L)),
        v((rows_s, D), BF16), v((1, D)), v((1, L)),
        v((dpn, rows_t, D), BF16), v((L, D), BF16), v((L, LANES)), v((H, L, ih)),
        v((Z, H, cb, ih), BF16), v((Z, H, cb, ih), BF16), v((H, cb, ih)), v((cb, ih), BF16), v((cb, ih), BF16),
        v((Z, H, 1, ih)), v((Z, H, 1, ih)), v((dpn, H, 1, ih)), v((Z, H, 1, ih)), v((Z, H, 1, ih)),
        v((H, 1, ih)), v((1, ih)),
        v((Z * C, rows_s // C, D), BF16), v((H, LANES // H, L), BF16), v((Z, cb, LANES), BF16),
        v((Z, cb, LANES), BF16), v((L, LANES)), v((dpn, 1, ih)), v((1, ih)), v((Z, 1, ih)), v((cb, ih)),
        v((L, LANES)), v((1, L)), v((Z, 1, L)), v((1, L)), v((1, L)),
        v((Z, cb, LANES), BF16), v((Z, cb, LANES), BF16), v((H, LANES // H, L)),
        v((LANES // H, L), BF16), v((LANES // H, L), BF16),
        v((dpn, 1, LANES)), v((1, LANES)), v((Z, 1, LANES)), v((1, LANES)), v((1, LANES)),
        pltpu.SemaphoreType.DMA((8,)), pltpu.SemaphoreType.DMA((dpn,)), pltpu.SemaphoreType.DMA((Z * C,)),
        pltpu.SemaphoreType.DMA((Z,)), pltpu.SemaphoreType.DMA((15,)), pltpu.SemaphoreType.DMA((18,)),
    ]
    vmem = pl.BlockSpec(memory_space=pltpu.VMEM)
    head_grad, bias_grad, loss = pl.pallas_call(
        functools.partial(step_kernel, sizes),
        out_shape=(
            jax.ShapeDtypeStruct((LANES // H, L), F32),
            jax.ShapeDtypeStruct((1, L), F32),
            jax.ShapeDtypeStruct((1, LANES), F32),
        ),
        in_specs=[pl.BlockSpec(memory_space=pl.ANY)] * 8,
        out_specs=(vmem, vmem, vmem),
        scratch_shapes=scratch,
        compiler_params=pltpu.CompilerParams(
            collective_id=0, has_side_effects=True, vmem_limit_bytes=67043328
        ),
    )(tf, tg, w, tb, sf, sg.reshape(1, -1), sh, sb.reshape(1, -1))
    return loss[0, 0], head_grad, bias_grad[0]


def solution(mesh, sizes=(8, 2, 4, 4, 2)):
    torus = Mesh(mesh.devices.reshape(sizes), AXES)
    placed = (
        P(MEMBER, DP, None),
        P(MEMBER, None),
        P(MEMBER, None, DP),
        P(MEMBER, DP),
        P(MEMBER, None),
        P(),
        P(MEMBER, DP),
        P(DP),
    )
    return jax.shard_map(
        functools.partial(on_device, sizes),
        mesh=torus,
        in_specs=placed,
        out_specs=(P(), P(MEMBER, DP), P(DP)),
        check_vma=False,
    )
```

time: 219 us -> 63.9 us (0.29)
  blocking collectives: 119 us -> 0 us
  Pallas kernels: 0 us -> 57.2 us
  waiting for transfers between devices: 53.8 us -> 0 us
  starting transfers between devices: 28.6 us -> 0 us
  other arithmetic: 6.17 us -> 0.6 us
  matrix products: 3.74 us -> 0 us
    psum x5 -> x0, blocking collectives: 60.6 us -> none  [by_axis(): shard = lax.psum(shard, axis)]
    all_to_all x3 -> x0, blocking collectives: 58.6 us -> none  [the longest x2 34.2 us: sent_to_all(): lax.all_to_all(jnp.broadcast_to(shard[None], (devices, *shard.shape)), ax...]
    pallas_call x0 -> x1, Pallas kernels: none -> 57.2 us  [on_device(): pl.pallas_call(functools.partial(step_kernel, sizes), out_shape=(jax.Shap...]
    all_to_all x4 -> x0, waiting for transfers between devices: 53.8 us -> none  [the longest x3 53.8 us: sent_to_all(): lax.all_to_all(jnp.broadcast_to(shard[None], (devices, *shard.shape)), ax...]
    all_to_all x4 -> x0, starting transfers between devices: 28.6 us -> none  [the longest x3 25 us: sent_to_all(): lax.all_to_all(jnp.broadcast_to(shard[None], (devices, *shard.shape)), ax...]
    reduce_sum x11 -> x0, other arithmetic: 3.74 us -> none  [the longest x2 1.14 us: norm_rows(): spread = jnp.mean(center * center, axis=-1, keepdims=True)]
    dot_general x3 -> x0, matrix products: 3.74 us -> none  [the longest x1 1.77 us: on_device(): lax.dot_general(columns, term_signal, (((0,), (0,)), ((), ())), precision...]
    unnamed x12 -> x5, local copies, waits for them, and re-layouts: 0.03 us -> 2.81 us
  transfers between devices with their start and end apart: 4 -> 0, of which waited for: 3 -> 0; matrix products, arithmetic and copies ran while one was open for 2% -> 0% of each run, Pallas kernels for 0% -> 0%
where the time goes in v1:
time: 63.9 us; the launch traced here: 63.6 us
  Pallas kernels  57.2 us (90%)
  local copies, waits for them, and re-layouts  4.06 us (6%)
  between operations  1.82 us (3%)
    pallas_call x1, Pallas kernels, on_device(): pl.pallas_call(functools.partial(step_kernel, sizes), out_shape=(jax.Shap...  57.2 us
    unnamed x5, local copies, waits for them, and re-layouts  2.81 us

profile of v1, /device:TPU:1, one launch (start us, length us, event | category | flops | bytes accessed | tf_op | source)
XLA Modules:
  0.0 63.6 jit_solution(1074647830418782276)
XLA Ops:
  0.6 1.2 %reshape.13.sb_h = f32[1,384]{1,0:T(1,128)} reshape(f32[384]{0:T(512)} %param.15) | data formatting | bytes 3072 | tf_op jit(solution)/shard_map/reshape | solution.py:397
  1.9 57.2 %shard_map.103 = (f32[64,384]{1,0:T(8,128)}, f32[1,384]{1,0:T(1,128)}, f32[1,128]{1,0:T(1,128)}) custom-call(bf16[1,16,1024]{2,1,0:T(8,128)(2,1)} %tf_h.1, f32[1,1024]{1,0:T(1,128)} %tg_h.1, bf16[1,1024,384]{2,1,0:T(8,128)(2,1)} %w_h.1, f32[1,384]{1,0:T(1,128)} %tb_h.1, bf16[32,1024]{1,0:T(8,128)(2,1)} %sf_h.1, f32[1,1024]{1,0:T(1,128)} %bitcast.3, ...), custom_call_target="tpu_custom_call" | custom-call | tf_op jit(solution)/shard_map/pallas_call | solution.py:384
  59.1 0.0 copy-start
  59.1 0.7 %copy-done = f32[1,384]{1,0:T(1,128)S(1)} copy-done((f32[1,384]{1,0:T(1,128)S(1)}, f32[1,384]{1,0:T(1,128)}, u32[]{:S(2)}) %copy-start) | copy-done | bytes 1560
  59.7 0.6 reduce
  60.3 0.0 copy-start.1
  60.3 0.6 copy-done.1
  61.0 1.5 %copy.14 = f32[64,384]{1,0:T(8,128)} copy(f32[64,384]{1,0:T(8,128)} %get-tuple-element.13) | data formatting | bytes 196608
Async XLA Ops:
  59.1 0.7 %copy-start = (f32[1,384]{1,0:T(1,128)S(1)}, f32[1,384]{1,0:T(1,128)}, u32[]{:S(2)}) copy-start(f32[1,384]{1,0:T(1,128)} %get-tuple-element.8) | copy-start | bytes 4612
  60.3 0.6 copy-start.1

commit v2 on v1

v2 whole, which is shorter than its diff:
```python
import functools

import jax
import jax.numpy as jnp
from jax import lax
from jax.experimental import pallas as pl
from jax.experimental.pallas import tpu as pltpu
from jax.sharding import Mesh
from jax.sharding import PartitionSpec as P

MEMBER = ("member_0", "member_1")
DP = ("dp_0", "dp_1", "dp_2")
AXES = MEMBER + DP
LANES = 128
F32 = jnp.float32
BF16 = jnp.bfloat16
NT = (((1,), (1,)), ((), ()))


def norm_rows(values, gain_row):
    values = values.astype(F32)
    center = values - jnp.mean(values, axis=-1, keepdims=True)
    spread = jnp.mean(center * center, axis=-1, keepdims=True)
    return center * lax.rsqrt(spread + 1e-06) * gain_row


def gamma_parts(x):
    small = x < 8.0
    base = jnp.where(small, x, 1.0)
    product = base
    harmonic = 1.0 / base
    for step in range(1, 8):
        product = product * (base + step)
        harmonic = harmonic + 1.0 / (base + step)
    big = jnp.where(small, x + 8.0, x)
    log_big = jnp.log(big)
    inv = 1.0 / big
    inv2 = inv * inv
    lgamma = (big - 0.5) * log_big - big + 0.9189385332046727
    lgamma = lgamma + inv * (1.0 / 12 - inv2 * (1.0 / 360 - inv2 * (1.0 / 1260)))
    digamma = log_big - 0.5 * inv - inv2 * (1.0 / 12 - inv2 * (1.0 / 120 - inv2 * (1.0 / 252)))
    lgamma = lgamma - jnp.where(small, jnp.log(product), 0.0)
    digamma = digamma - jnp.where(small, harmonic, 0.0)
    return lgamma, digamma


def start_copy(src, dst, send_sem, recv_sem, device):
    pltpu.make_async_remote_copy(
        src_ref=src,
        dst_ref=dst,
        send_sem=send_sem,
        recv_sem=recv_sem,
        device_id=device,
        device_id_type=pl.DeviceIdType.MESH,
    ).start()


def wait_bytes(ref, sem):
    pltpu.make_async_copy(ref, ref, sem).wait()


def step_kernel(
    sizes,
    tf_h, tg_h, w_h, tb_h, sf_h, sg_h, sh_h, sb_h,
    hg_o, bias_o, loss_o,
    tfv, tgv, wv, tbv, sfv, sgv, sbv, shv,
    xn, wt, tbt, lg, send, rb, tz, tb_s, tp,
    bm, bs, st, vs, vr,
    sn, sws, swr, swp, swq, swx, sbt, ad, asum, az, al_s,
    bc, bg_s, bgr, bh, bp, hs, hr, ht, hb, hp,
    ld, lz,
    in_sems, xn_sems, sn_sems, rb_sems, one, out,
):
    Z, H, Y, X, C = sizes
    z, h, y, x, c = (lax.axis_index(a) for a in AXES)
    dpn = Y * X * C
    me = (y * X + x) * C + c
    D = xn.shape[2]
    rows_t = xn.shape[1]
    L = wt.shape[0]
    cb = L // Z
    half_blocks = dpn // H
    ih = half_blocks * rows_t
    qb = half_blocks // 2
    iq = ih // 2
    rows_s = ih // Z
    q = rows_s // rows_t
    images = ih * H
    lane_half = LANES // H

    def at(nz=None, nh=None, ny=None, nx=None, nc=None):
        new = (nz, nh, ny, nx, nc)
        return tuple(old if n is None else n for old, n in zip((z, h, y, x, c), new))

    def spot(py, px, pc):
        d = (py * X + px) * C + pc
        m = d // q
        return (m % H) * half_blocks + (m // H) * q + d % q

    def ring(k):
        return lax.rem(z + k, Z)

    z_order = sorted(range(1, Z), key=lambda k: -min(k, Z - k))
    plane = [
        (lax.rem(y + i, Y), lax.rem(x + j, X), lax.rem(c + k, C))
        for i in reversed(range(Y))
        for j in range(X)
        for k in range(C)
        if i or j or k
    ]
    column = [y]
    if Y > 1:
        column.append(y + 1 - 2 * (y % 2))
    for k in range(2, Y):
        column.append((column[k - 2] + 2) % Y)
    groups = [range(0, Y // 2), range(Y // 2, Y)]
    first, second = groups
    near = [k for k in first if k]
    row_out = [lax.rem(x + j, X) for j in (2, 1, 3) if j < X]
    row_in = [lax.rem(x + j, X) for j in (1, 3, 2) if j < X]
    other = [lax.rem(c + e, C) for e in range(1, C)]

    loads = [
        pltpu.make_async_copy(src, dst, in_sems.at[i])
        for i, (src, dst) in enumerate(
            [
                (tf_h.at[0], tfv),
                (tg_h, tgv),
                (sf_h, sfv),
                (sg_h, sgv),
                (sh_h, shv),
                (tb_h, tbv),
                (sb_h, sbv),
                (w_h.at[0], wv),
            ]
        )
    ]
    for load in loads:
        load.start()
    barrier = pltpu.get_barrier_semaphore()
    peers = [at(ny=column[k]) for k in range(1, Y)] + [at(nx=px) for px in row_out]
    peers += [at(ny=column[k], nx=px) for k in near for px in row_out]
    peers += [at(nc=e) for e in other] + [at(nz=ring(k)) for k in range(1, Z)] + [at(nh=1 - h)]
    for peer in peers:
        pl.semaphore_signal(barrier, 1, device_id=peer, device_id_type=pl.DeviceIdType.MESH)

    own = spot(y, x, c)
    loads[0].wait()
    loads[1].wait()
    xn[own] = norm_rows(tfv[...], tgv[...]).astype(BF16)
    loads[2].wait()
    loads[3].wait()
    normed_s = norm_rows(sfv[...], sgv[...].reshape(1, D)).astype(BF16)
    sn[pl.ds(z * C, C)] = normed_s.reshape(C, rows_s // C, D)
    loads[4].wait()
    head = shv[...].astype(F32)
    blank = jnp.zeros_like(head)
    head = jnp.concatenate(
        [jnp.where(h == i, head, blank) for i in range(H)], axis=0
    ).T
    sws[...] = head.astype(BF16).reshape(Z, cb, LANES)
    pl.semaphore_wait(barrier, len(peers))

    def forward(block, device):
        start_copy(xn.at[block], xn.at[block], out.at[0], xn_sems.at[block], device)

    def arrived(block):
        wait_bytes(xn.at[block], xn_sems.at[block])

    def to_core(block):
        for e in other:
            forward(block, at(nc=e))

    for k in list(second) + near:
        forward(own, at(ny=column[k]))
    for k in [0] + near:
        for px in row_out:
            forward(own, at(ny=column[k], nx=px))
    to_core(own)
    for k in z_order:
        start_copy(sws.at[ring(k)], swr.at[z], out.at[3], one.at[1], at(nz=ring(k)))
    mine = z * C + c
    for k in z_order:
        start_copy(sn.at[mine], sn.at[mine], out.at[2], sn_sems.at[mine], at(nz=ring(k)))
    swr[z] = sws[z]

    loads[5].wait()
    loads[6].wait()
    tbt[...] = jnp.broadcast_to(tbv[...], (LANES, L)).T
    sbt[...] = jnp.broadcast_to(sbv[...].reshape(1, L), (LANES, L)).T
    loads[7].wait()
    for k in range(D // LANES):
        part = slice(k * LANES, (k + 1) * LANES)
        wt[:, part] = wv[part, :].astype(F32).T.astype(BF16)

    def from_core(k):
        for e in other:
            for px in [x] + row_in:
                arrived(spot(column[k], px, e))

    def logits_of(group):
        b = column[groups[group][0]] // (Y // 2)
        held = jnp.concatenate(
            [xn[pl.ds(a * half_blocks + b * qb, qb)].reshape(iq, D) for a in range(H)], axis=0
        )
        lg[...] = lax.dot_general(wt[...], held, NT, preferred_element_type=F32)
        for k in z_order + [0]:
            to = ring(k)
            rows = pl.ds(pl.multiple_of(to * cb, 16), cb)
            part = lg[rows, :] + tbt[rows, 0:1]
            top = jnp.max(part, axis=0, keepdims=True)
            part = part - top
            send[b, to] = part.astype(BF16)
            bm[b, to] = top
            bs[b, to] = jnp.sum(jnp.exp(part), axis=0, keepdims=True)
            if k:
                start_copy(send.at[b, to], rb.at[b, z], out.at[4 + 14 * group], rb_sems.at[group], at(nz=to))

    def pair_head():
        wait_bytes(swr.at[pl.ds(0, Z - 1)], one.at[1])
        for j in range(Z // 2):
            turned = pltpu.roll(swr[j + Z // 2].astype(F32), lane_half, 1)
            swp[j] = (swr[j].astype(F32) + turned).astype(BF16)
        start_copy(swp, swq, out.at[1], one.at[0], at(nh=1 - h))

    for k in near:
        block = spot(column[k], x, c)
        arrived(block)
        to_core(block)
    for k in second:
        block = spot(column[k], x, c)
        arrived(block)
        for px in row_out:
            forward(block, at(nx=px))
        to_core(block)
    for k in first:
        for px in row_in:
            block = spot(column[k], px, c)
            arrived(block)
            to_core(block)
    pair_head()
    for k in first:
        from_core(k)
    logits_of(0)
    for k in range(1, Z):
        block = ring(k) * C + c
        wait_bytes(sn.at[block], sn_sems.at[block])
        for e in other:
            start_copy(sn.at[block], sn.at[block], out.at[2], sn_sems.at[block], at(nc=e))
    for k in second:
        for px in row_in:
            block = spot(column[k], px, c)
            arrived(block)
            to_core(block)
    for k in second:
        from_core(k)
    logits_of(1)
    tops = bm[...]
    top = jnp.max(tops, axis=1)
    st[me] = top + jnp.log(jnp.sum(bs[...] * jnp.exp(tops - top[:, None]), axis=1))
    for a, b, e in plane:
        start_copy(st.at[me], st.at[me], out.at[5], one.at[2], at(ny=a, nx=b, nc=e))

    for e in other:
        for k in range(1, Z):
            block = ring(k) * C + e
            wait_bytes(sn.at[block], sn_sems.at[block])
    wait_bytes(swq, one.at[0])
    lane = lax.broadcasted_iota(jnp.int32, (cb, LANES), 1)
    theirs = jnp.where(lane >= lane_half, 1, 0) != h
    for j in range(Z // 2):
        packed = swq[j].astype(F32)
        turned = pltpu.roll(packed, lane_half, 1)
        for i, value in ((j, packed), (j + Z // 2, turned)):
            swx[i] = jnp.where(theirs, value, swr[i].astype(F32)).astype(BF16)
    scores = jnp.zeros((cb, ih), F32)
    for k in range(Z):
        part = slice(k * LANES, (k + 1) * LANES)
        scores = scores + lax.dot_general(
            swx[k], sn[:, :, part].reshape(ih, LANES), NT, preferred_element_type=F32
        )
    my_rows = pl.ds(pl.multiple_of(z * cb, 16), cb)
    alphas = jnp.exp(scores + sbt[my_rows, 0:1])
    al_s[...] = alphas
    ad[me] = jnp.sum(alphas, axis=0, keepdims=True)
    for a, b, e in plane:
        start_copy(ad.at[me], ad.at[me], out.at[6], one.at[3], at(ny=a, nx=b, nc=e))

    wait_bytes(st.at[pl.ds(0, dpn - 1)], one.at[2])
    tops = st[...]
    top = jnp.max(tops, axis=0)
    log_norm = top + jnp.log(jnp.sum(jnp.exp(tops - top[None]), axis=0))
    mine = z * H + h
    for b in range(2):
        shift = bm[b] - log_norm[b][None]
        for a in range(H):
            vs[:, a, b] = shift[:, :, a * iq : (a + 1) * iq]
    for k in z_order + [0]:
        start_copy(vs.at[ring(k), 1 - h], vr.at[mine], out.at[7], one.at[4], at(nz=ring(k), nh=1 - h))
    for k in z_order:
        start_copy(vs.at[ring(k), h], vr.at[mine], out.at[7], one.at[4], at(nz=ring(k)))
    vr[mine] = vs[z, h]

    wait_bytes(ad.at[pl.ds(0, dpn - 1)], one.at[3])
    asum[...] = jnp.sum(ad[...], axis=0)
    for k in z_order:
        start_copy(asum, az.at[z], out.at[8], one.at[5], at(nz=ring(k)))
    az[z] = asum[...]
    lgamma, digamma = gamma_parts(al_s[...])

    for group in range(2):
        b = column[groups[group][0]] // (Y // 2)
        wait_bytes(rb.at[b, pl.ds(0, Z - 1)], rb_sems.at[group])
        rb[b, z] = send[b, z]
        total = jnp.sum(rb[b].astype(F32), axis=0)
        for a in range(H):
            tz[a, b] = total[:, a * iq : (a + 1) * iq]
        tb_s[b] = tz[1 - h, b].astype(BF16)
        start_copy(tb_s.at[b], tp.at[b], out.at[9], one.at[6], at(nh=1 - h))
    wait_bytes(az.at[pl.ds(0, Z - 1)], one.at[5])
    lgamma_sum, digamma_sum = gamma_parts(jnp.sum(az[...], axis=0))
    wait_bytes(tp, one.at[6])
    wait_bytes(vr.at[pl.ds(0, Z * H - 1)], one.at[4])
    shift = jnp.sum(vr[...], axis=0)
    target = jnp.concatenate(
        [tz[h, b] + tp[b].astype(F32) + shift[b] for b in range(2)], axis=1
    ) / (Z * H)

    alphas = al_s[...]
    signal = alphas * (digamma - digamma_sum - target)
    terms = jnp.sum(lgamma - (alphas - 1.0) * target, axis=0, keepdims=True)
    terms = terms - lgamma_sum / (Z * dpn)
    deep = z * C + c
    ld[deep] = jnp.broadcast_to(jnp.sum(terms, axis=1, keepdims=True), (1, LANES))
    for k in z_order + [0]:
        for e in other + ([c] if k else []):
            start_copy(ld.at[deep], ld.at[deep], out.at[11], one.at[8], at(nz=ring(k), nc=e))

    high = signal.astype(BF16)
    rest = signal - high.astype(F32)
    mid = rest.astype(BF16)
    low = (rest - mid.astype(F32)).astype(BF16)
    parts = lax.dot_general(
        jnp.concatenate([high, mid, low], axis=0),
        sn[...].reshape(ih, D),
        (((1,), (0,)), ((), ())),
        preferred_element_type=F32,
    )
    grad = parts[:cb] + parts[cb : 2 * cb] + parts[2 * cb :]
    for k in range(Z):
        hs[k] = grad[:, k * LANES : (k + 1) * LANES].astype(BF16)
    for k in z_order:
        start_copy(hs.at[ring(k)], hr.at[z], out.at[12], one.at[9], at(nz=ring(k)))
    hr[z] = hs[z]
    bc[...] = jnp.zeros_like(bc)
    bc[my_rows, :] = jnp.broadcast_to(jnp.sum(signal, axis=1, keepdims=True), (cb, LANES))
    bg_s[...] = bc[...].T[0:1]
    for k in z_order:
        start_copy(bg_s, bgr.at[z], out.at[13], one.at[10], at(nz=ring(k)))
    bgr[z] = bg_s[...]

    wait_bytes(ld.at[pl.ds(0, Z * C - 1)], one.at[8])
    wide = (h * Y + y) * X + x
    lz[wide] = jnp.sum(ld[...], axis=0)
    for ph in (1 - h, h):
        for k in reversed(range(Y)):
            for px in row_out + ([x] if k or ph is not h else []):
                start_copy(lz.at[wide], lz.at[wide], out.at[14], one.at[11], at(nh=ph, ny=column[k], nx=px))

    wait_bytes(hr.at[pl.ds(0, Z - 1)], one.at[9])
    rows = hr[...].astype(F32).reshape(L, LANES).T
    ht[...] = rows.reshape(H, lane_half, L)
    hb[...] = ht[1 - h].astype(BF16)
    start_copy(hb, hp, out.at[15], one.at[12], at(nh=1 - h))
    wait_bytes(bgr.at[pl.ds(0, Z - 1)], one.at[10])
    bh[...] = jnp.sum(bgr[...], axis=0)
    start_copy(bh, bp, out.at[16], one.at[13], at(nh=1 - h))
    wait_bytes(hp, one.at[12])
    hg_o[...] = ht[h] + hp[...].astype(F32)
    wait_bytes(bp, one.at[13])
    bias_o[...] = ((bh[...] + bp[...]) / images).reshape(L)
    wait_bytes(lz.at[pl.ds(0, H * Y * X - 1)], one.at[11])
    loss_o[...] = jnp.sum(lz[...], axis=0) / (images * (L * dpn))

    sent = {
        0: xn.at[pl.ds(0, dpn - 1)],
        1: swp,
        2: sn.at[pl.ds(0, (Z - 1) * C)],
        3: sws.at[pl.ds(0, Z - 1)],
        4: send.at[0, pl.ds(0, Z - 1)],
        5: st.at[pl.ds(0, dpn - 1)],
        6: ad.at[pl.ds(0, dpn - 1)],
        7: vr.at[pl.ds(0, Z * H - 1)],
        8: az.at[pl.ds(0, Z - 1)],
        9: tb_s,
        11: ld.at[pl.ds(0, Z * C - 1)],
        12: hs.at[pl.ds(0, Z - 1)],
        13: bgr.at[pl.ds(0, Z - 1)],
        14: lz.at[pl.ds(0, H * Y * X - 1)],
        15: hb,
        16: bh,
        18: send.at[1, pl.ds(0, Z - 1)],
    }
    for i, ref in sent.items():
        wait_bytes(ref, out.at[i])


def on_device(sizes, tf, tg, w, tb, sf, sg, sh, sb):
    Z, H, Y, X, C = sizes
    dpn = Y * X * C
    rows_t, D = tf.shape[1:]
    L = w.shape[2]
    cb = L // Z
    ih = rows_t * dpn // H
    iq = ih // 2
    rows_s = sf.shape[0]
    images = ih * H
    assert D == Z * LANES and rows_s * Z == ih and sh.shape[0] * H == LANES

    def v(shape, dtype=F32):
        return pltpu.VMEM(shape, dtype)

    scratch = [
        v((rows_t, D), BF16), v((1, D)), v((D, L), BF16), v((1, L)),
        v((rows_s, D), BF16), v((D,)), v((L,)), v((LANES // H, L), BF16),
        v((dpn, rows_t, D), BF16), v((L, D), BF16), v((L, LANES)), v((L, ih)),
        v((2, Z, cb, ih), BF16), v((2, Z, cb, ih), BF16), v((H, 2, cb, iq)), v((2, cb, iq), BF16), v((2, cb, iq), BF16),
        v((2, Z, 1, ih)), v((2, Z, 1, ih)), v((dpn, 2, 1, ih)), v((Z, H, 2, 1, iq)), v((Z * H, 2, 1, iq)),
        v((Z * C, rows_s // C, D), BF16), v((Z, cb, LANES), BF16), v((Z, cb, LANES), BF16),
        v((Z // 2, cb, LANES), BF16), v((Z // 2, cb, LANES), BF16), v((Z, cb, LANES), BF16),
        v((L, LANES)), v((dpn, 1, ih)), v((1, ih)), v((Z, 1, ih)), v((cb, ih)),
        v((L, LANES)), v((1, L)), v((Z, 1, L)), v((1, L)), v((1, L)),
        v((Z, cb, LANES), BF16), v((Z, cb, LANES), BF16), v((H, LANES // H, L)),
        v((LANES // H, L), BF16), v((LANES // H, L), BF16),
        v((Z * C, 1, LANES)), v((H * Y * X, 1, LANES)),
        pltpu.SemaphoreType.DMA((8,)), pltpu.SemaphoreType.DMA((dpn,)), pltpu.SemaphoreType.DMA((Z * C,)),
        pltpu.SemaphoreType.DMA((2,)), pltpu.SemaphoreType.DMA((15,)), pltpu.SemaphoreType.DMA((19,)),
    ]
    vmem = pl.BlockSpec(memory_space=pltpu.VMEM)
    head_grad, bias_grad, loss = pl.pallas_call(
        functools.partial(step_kernel, sizes),
        out_shape=(
            jax.ShapeDtypeStruct((LANES // H, L), F32),
            jax.ShapeDtypeStruct((L,), F32),
            jax.ShapeDtypeStruct((1, LANES), F32),
        ),
        in_specs=[pl.BlockSpec(memory_space=pl.ANY)] * 8,
        out_specs=(vmem, vmem, vmem),
        scratch_shapes=scratch,
        compiler_params=pltpu.CompilerParams(
            collective_id=0, has_side_effects=True, vmem_limit_bytes=67043328
        ),
    )(tf, tg, w, tb, sf, sg, sh, sb)
    return loss[0, 0], head_grad / images, bias_grad


def solution(mesh, sizes=(8, 2, 4, 4, 2)):
    torus = Mesh(mesh.devices.reshape(sizes), AXES)
    placed = (
        P(MEMBER, DP, None),
        P(MEMBER, None),
        P(MEMBER, None, DP),
        P(MEMBER, DP),
        P(MEMBER, None),
        P(),
        P(MEMBER, DP),
        P(DP),
    )
    return jax.shard_map(
        functools.partial(on_device, sizes),
        mesh=torus,
        in_specs=placed,
        out_specs=(P(), P(MEMBER, DP), P(DP)),
        check_vma=False,
    )
```

time: 63.9 us -> 56.1 us (0.88)
  Pallas kernels: 57.2 us -> 51.9 us
  local copies, waits for them, and re-layouts: 4.06 us -> 0.59 us
  other arithmetic: 0.6 us -> 1.54 us
    pallas_call x1, Pallas kernels: 57.2 us -> 51.9 us  [on_device(): pl.pallas_call(functools.partial(step_kernel, sizes), out_shape=(jax.Shap...]
    unnamed x5, local copies, waits for them, and re-layouts: 2.81 us -> 0.59 us
    div x0 -> x1, other arithmetic: none -> 1.54 us  [on_device(): return (loss[0, 0], head_grad / images, bias_grad)]
    reshape x1 -> x0, local copies, waits for them, and re-layouts: 1.25 us -> none  [on_device(): sb.reshape(1, -1)]
where the time goes in v2:
time: 56.1 us; the launch traced here: 55.9 us
  Pallas kernels  51.9 us (93%)
  between operations  1.84 us (3%)
  other arithmetic  1.54 us (3%)
  local copies, waits for them, and re-layouts  0.59 us (1%)
    pallas_call x1, Pallas kernels, on_device(): pl.pallas_call(functools.partial(step_kernel, sizes), out_shape=(jax.Shap...  51.9 us
    div x1, other arithmetic, on_device(): return (loss[0, 0], head_grad / images, bias_grad)  1.54 us

profile of v2, /device:TPU:1, one launch (start us, length us, event | category | flops | bytes accessed | tf_op | source)
XLA Modules:
  0.0 55.9 jit_solution(6248877738816976514)
XLA Ops:
  0.6 51.9 %shard_map.103 = (f32[64,384]{1,0:T(8,128)}, f32[384]{0:T(512)}, f32[1,128]{1,0:T(1,128)}) custom-call(bf16[1,16,1024]{2,1,0:T(8,128)(2,1)} %tf_h.1, f32[1,1024]{1,0:T(1,128)} %tg_h.1, bf16[1,1024,384]{2,1,0:T(8,128)(2,1)} %w_h.1, f32[1,384]{1,0:T(1,128)} %tb_h.1, bf16[32,1024]{1,0:T(8,128)(2,1)} %sf_h.1, f32[1024]{0:T(1024)} %sg_h.1, bf16[64,384]{1,0:T(8,128)(2,1)} %sh_h.1, ...), custom_call_target="tpu_custom_call" | custom-call | tf_op jit(solution)/shard_map/pallas_call | solution.py:440
  52.5 0.0 copy-start.1
  52.6 0.0 copy-start
  52.6 1.5 %broadcast_multiply_fusion = f32[64,384]{1,0:T(8,128)} fusion(f32[64,384]{1,0:T(8,128)} %get-tuple-element.7), kind=kLoop, calls=%fused_computation | loop fusion | flops 24576 | bytes 196608 | tf_op jit(solution)/shard_map/div | solution.py:454
  54.1 0.0 copy-done.1
  54.2 0.0 copy-done
  54.2 0.6 %copy.14 = f32[384]{0:T(512)} copy(f32[384]{0:T(512)S(1)} %copy-done) | data formatting | bytes 3072
Async XLA Ops:
  52.5 1.6 %copy-start.1 = (f32[1,128]{1,0:T(1,128)S(1)}, f32[1,128]{1,0:T(1,128)}, u32[]{:S(2)}) copy-start(f32[1,128]{1,0:T(1,128)} %get-tuple-element.6) | copy-start | bytes 1540
  52.6 1.6 %copy-start = (f32[384]{0:T(512)S(1)}, f32[384]{0:T(512)}, u32[]{:S(2)}) copy-start(f32[384]{0:T(512)} %get-tuple-element.14) | copy-start | bytes 4612

commit v3 on v2

--- a/solution.py
+++ b/solution.py
@@ -203,18 +203,21 @@
         held = jnp.concatenate(
             [xn[pl.ds(a * half_blocks + b * qb, qb)].reshape(iq, D) for a in range(H)], axis=0
         )
-        lg[...] = lax.dot_general(wt[...], held, NT, preferred_element_type=F32)
-        for k in z_order + [0]:
-            to = ring(k)
-            rows = pl.ds(pl.multiple_of(to * cb, 16), cb)
+        for part in (slice(0, L // 2), slice(L // 2, L)):
+            lg[part, :] = lax.dot_general(wt[part, :], held, NT, preferred_element_type=F32)
+        for to in range(Z):
+            rows = slice(to * cb, (to + 1) * cb)
             part = lg[rows, :] + tbt[rows, 0:1]
             top = jnp.max(part, axis=0, keepdims=True)
             part = part - top
             send[b, to] = part.astype(BF16)
             bm[b, to] = top
             bs[b, to] = jnp.sum(jnp.exp(part), axis=0, keepdims=True)
-            if k:
-                start_copy(send.at[b, to], rb.at[b, z], out.at[4 + 14 * group], rb_sems.at[group], at(nz=to))
+        for k in z_order:
+            to = ring(k)
+            start_copy(
+                send.at[b, to], rb.at[b, z], out.at[4 + 14 * group], rb_sems.at[group], at(nz=to)
+            )
 
     def pair_head():
         wait_bytes(swr.at[pl.ds(0, Z - 1)], one.at[1])
@@ -223,15 +226,12 @@
             swp[j] = (swr[j].astype(F32) + turned).astype(BF16)
         start_copy(swp, swq, out.at[1], one.at[0], at(nh=1 - h))
 
-    for k in near:
+    for k in list(second) + near:
         block = spot(column[k], x, c)
         arrived(block)
-        to_core(block)
-    for k in second:
-        block = spot(column[k], x, c)
-        arrived(block)
-        for px in row_out:
-            forward(block, at(nx=px))
+        if k in second:
+            for px in row_out:
+                forward(block, at(nx=px))
         to_core(block)
     for k in first:
         for px in row_in:
@@ -242,16 +242,16 @@
     for k in first:
         from_core(k)
     logits_of(0)
+    for k in second:
+        for px in row_in:
+            block = spot(column[k], px, c)
+            arrived(block)
+            to_core(block)
     for k in range(1, Z):
         block = ring(k) * C + c
         wait_bytes(sn.at[block], sn_sems.at[block])
         for e in other:
             start_copy(sn.at[block], sn.at[block], out.at[2], sn_sems.at[block], at(nc=e))
-    for k in second:
-        for px in row_in:
-            block = spot(column[k], px, c)
-            arrived(block)
-            to_core(block)
     for k in second:
         from_core(k)
     logits_of(1)
@@ -448,9 +448,9 @@
         out_specs=(vmem, vmem, vmem),
         scratch_shapes=scratch,
         compiler_params=pltpu.CompilerParams(
-            collective_id=0, has_side_effects=True, vmem_limit_bytes=67043328
+            collective_id=0, has_side_effects=True, vmem_limit_bytes=48 * 2**20
         ),
-    )(tf, tg, w, tb, sf, sg, sh, sb)
+    )(*(pltpu.with_memory_space_constraint(a, pltpu.HBM) for a in (tf, tg, w, tb, sf, sg, sh, sb)))
     return loss[0, 0], head_grad / images, bias_grad
 
 

time: 56.1 us -> 52.6 us (0.938)
  the two profiles are of different devices: /device:TPU:1 before, /device:TPU:8 now
where the time goes in v3:
time: 52.6 us; the launch traced here: 52.5 us
  Pallas kernels  49.4 us (94%)
  between operations  1.81 us (3%)
  other arithmetic  0.65 us (1%)
  local copies, waits for them, and re-layouts  0.58 us (1%)
    pallas_call x1, Pallas kernels, on_device(): pl.pallas_call(functools.partial(step_kernel, sizes), out_shape=(jax.Shap...  49.4 us

profile of v3, /device:TPU:8, one launch (start us, length us, event | category | flops | bytes accessed | tf_op | source)
XLA Modules:
  0.0 52.5 jit_solution(524271318309300722)
XLA Ops:
  0.6 49.4 %shard_map.103 = (f32[64,384]{1,0:T(8,128)S(1)}, f32[384]{0:T(512)S(1)}, f32[1,128]{1,0:T(1,128)S(1)}) custom-call(bf16[1,16,1024]{2,1,0:T(8,128)(2,1)} %tf_h.1, f32[1,1024]{1,0:T(1,128)} %tg_h.1, bf16[1,1024,384]{2,1,0:T(8,128)(2,1)} %w_h.1, f32[1,384]{1,0:T(1,128)} %tb_h.1, bf16[32,1024]{1,0:T(8,128)(2,1)} %sf_h.1, f32[1024]{0:T(1024)} %sg_h.1, ...), custom_call_target="tpu_custom_call" | custom-call | tf_op jit(solution)/shard_map/pallas_call | solution.py:440
  50.1 0.6 %broadcast_multiply_fusion = f32[64,384]{1,0:T(8,128)} fusion(f32[64,384]{1,0:T(8,128)S(1)} %get-tuple-element.7), kind=kLoop, calls=%fused_computation | loop fusion | flops 24576 | bytes 196608 | tf_op jit(solution)/shard_map/div | solution.py:454
  50.8 0.6 %copy.14 = f32[384]{0:T(512)} copy(f32[384]{0:T(512)S(1)} %get-tuple-element.14) | data formatting | bytes 3072

commit v4 on v3

v4 whole, which is shorter than its diff:
```python
import functools
import math

import jax
import jax.numpy as jnp
from jax import lax
from jax.experimental import pallas as pl
from jax.experimental.pallas import tpu as pltpu
from jax.sharding import Mesh
from jax.sharding import PartitionSpec as P

MEMBER = ("member_0", "member_1")
DP = ("dp_0", "dp_1", "dp_2")
AXES = MEMBER + DP
LANES = 128
F32 = jnp.float32
BF16 = jnp.bfloat16
NT = (((1,), (1,)), ((), ()))


def norm_rows(values, gain_row):
    values = values.astype(F32)
    center = values - jnp.mean(values, axis=-1, keepdims=True)
    spread = jnp.mean(center * center, axis=-1, keepdims=True)
    return center * lax.rsqrt(spread + 1e-06) * gain_row


def gamma_parts(x):
    small = x < 8.0
    base = jnp.where(small, x, 1.0)
    product = base
    harmonic = 1.0 / base
    for step in range(1, 8):
        product = product * (base + step)
        harmonic = harmonic + 1.0 / (base + step)
    big = jnp.where(small, x + 8.0, x)
    log_big = jnp.log(big)
    inv = 1.0 / big
    inv2 = inv * inv
    lgamma = (big - 0.5) * log_big - big + 0.9189385332046727
    lgamma = lgamma + inv * (1.0 / 12 - inv2 * (1.0 / 360 - inv2 * (1.0 / 1260)))
    digamma = log_big - 0.5 * inv - inv2 * (1.0 / 12 - inv2 * (1.0 / 120 - inv2 * (1.0 / 252)))
    lgamma = lgamma - jnp.where(small, jnp.log(product), 0.0)
    digamma = digamma - jnp.where(small, harmonic, 0.0)
    return lgamma, digamma


def wait_bytes(ref, sem):
    pltpu.make_async_copy(ref, ref, sem).wait()


def step_kernel(
    sizes,
    tf_h, tg_h, w_h, tb_h, sf_h, sg_h, sh_h, sb_h,
    hg_o, bias_o, loss_o,
    tfv, tgv, wv, tbv, sfv, sgv, sbv, shv,
    xn, wt, tbt, lg, send, rb, tz, tb_s, tp,
    bm, st, vs, vr,
    sn, sws, swr, swp, swq, swx, sbt, ad, asum, az, al_s,
    bc, bg_s, bgr, bh, bp, hs, hr, ht, hb, hp,
    ld, lz,
    tally, in_sems, xn_sems, core_sems, sn_sems, rb_sems, st_sems, one, out_sems,
):
    Z, H, Y, X, C = sizes
    z, h, y, x, c = (lax.axis_index(a) for a in AXES)
    dpn = Y * X * C
    me = (y * X + x) * C + c
    D = xn.shape[2]
    rows_t = xn.shape[1]
    L = wt.shape[0]
    cb = L // Z
    half_blocks = dpn // H
    ih = half_blocks * rows_t
    qb = half_blocks // 2
    iq = ih // 2
    rows_s = ih // Z
    q = rows_s // rows_t
    images = ih * H
    lane_half = LANES // H

    sent = []
    out = out_sems.at[0]

    def start_copy(src, dst, recv_sem, device):
        sent.append(math.prod(src.shape) * src.dtype.itemsize)
        pltpu.make_async_remote_copy(
            src_ref=src,
            dst_ref=dst,
            send_sem=out,
            recv_sem=recv_sem,
            device_id=device,
            device_id_type=pl.DeviceIdType.MESH,
        ).start()

    def wait_sum(sizes, sem):
        wait_bytes(tally.at[pl.ds(0, sum(sizes) // (2 * LANES))], sem)

    def at(nz=None, nh=None, ny=None, nx=None, nc=None):
        new = (nz, nh, ny, nx, nc)
        return tuple(old if n is None else n for old, n in zip((z, h, y, x, c), new))

    def spot(py, px, pc):
        d = (py * X + px) * C + pc
        m = d // q
        return (m % H) * half_blocks + (m // H) * q + d % q

    def ring(k):
        return lax.rem(z + k, Z)

    z_order = sorted(range(1, Z), key=lambda k: -min(k, Z - k))
    plane = [
        (lax.rem(y + i, Y), lax.rem(x + j, X), lax.rem(c + k, C))
        for i in reversed(range(Y))
        for j in range(X)
        for k in range(C)
        if i or j or k
    ]
    column = [y]
    if Y > 1:
        column.append(y + 1 - 2 * (y % 2))
    for k in range(2, Y):
        column.append((column[k - 2] + 2) % Y)
    groups = [range(0, Y // 2), range(Y // 2, Y)]
    first, second = groups
    near = [k for k in first if k]
    row_out = [lax.rem(x + j, X) for j in (2, 1, 3) if j < X]
    row_in = [lax.rem(x + j, X) for j in (1, 3, 2) if j < X]
    other = [lax.rem(c + e, C) for e in range(1, C)]

    loads = []
    for i, group in enumerate(
        [
            [(tf_h.at[0], tfv), (tg_h, tgv)],
            [(sf_h, sfv), (sg_h, sgv), (sh_h, shv)],
            [(tb_h, tbv), (sb_h, sbv), (w_h.at[0], wv)],
        ]
    ):
        for src, dst in group:
            pltpu.make_async_copy(src, dst, in_sems.at[i]).start()
        loads.append([math.prod(dst.shape) * dst.dtype.itemsize for _, dst in group])
    barrier = pltpu.get_barrier_semaphore()
    peers = [at(ny=column[k]) for k in range(1, Y)] + [at(nx=px) for px in row_out]
    peers += [at(ny=column[k], nx=px) for k in near for px in row_out]
    peers += [at(nc=e) for e in other] + [at(nz=ring(k)) for k in range(1, Z)] + [at(nh=1 - h)]
    for peer in peers:
        pl.semaphore_signal(barrier, 1, device_id=peer, device_id_type=pl.DeviceIdType.MESH)

    own = spot(y, x, c)
    wait_sum(loads[0], in_sems.at[0])
    xn[own] = norm_rows(tfv[...], tgv[...]).astype(BF16)
    pl.semaphore_wait(barrier, len(peers))

    def forward(k, px, device):
        block = spot(column[k], px, c)
        start_copy(xn.at[block], xn.at[block], xn_sems.at[column[k] * X + px], device)

    def arrived(k, px):
        wait_bytes(xn.at[spot(column[k], px, c)], xn_sems.at[column[k] * X + px])

    def to_core(k, px):
        block = spot(column[k], px, c)
        for e in other:
            start_copy(xn.at[block], xn.at[block], core_sems.at[int(k in second)], at(nc=e))

    for k in list(second) + near:
        forward(0, x, at(ny=column[k]))
    for k in [0] + near:
        for px in row_out:
            forward(0, x, at(ny=column[k], nx=px))
    to_core(0, x)
    wait_sum(loads[1], in_sems.at[1])
    head = shv[...].astype(F32)
    blank = jnp.zeros_like(head)
    head = jnp.concatenate([jnp.where(h == i, head, blank) for i in range(H)], axis=0).T
    sws[...] = head.astype(BF16).reshape(Z, cb, LANES)
    for k in z_order:
        start_copy(sws.at[ring(k)], swr.at[z], one.at[1], at(nz=ring(k)))
    swr[z] = sws[z]
    normed_s = norm_rows(sfv[...], sgv[...].reshape(1, D)).astype(BF16)
    sn[pl.ds(z * C, C)] = normed_s.reshape(C, rows_s // C, D)
    mine = z * C + c
    for k in z_order:
        start_copy(sn.at[mine], sn.at[mine], sn_sems.at[z], at(nz=ring(k)))

    wait_sum(loads[2], in_sems.at[2])
    tbt[...] = jnp.broadcast_to(tbv[...], (LANES, L)).T
    sbt[...] = jnp.broadcast_to(sbv[...].reshape(1, L), (LANES, L)).T
    for k in range(D // LANES):
        part = slice(k * LANES, (k + 1) * LANES)
        wt[:, part] = wv[part, :].astype(F32).T.astype(BF16)

    def from_core(group):
        if other:
            wait_bytes(xn.at[pl.ds(0, len(groups[group]) * X)], core_sems.at[group])

    def logits_of(group):
        b = column[groups[group][0]] // (Y // 2)
        held = jnp.concatenate(
            [xn[pl.ds(a * half_blocks + b * qb, qb)].reshape(iq, D) for a in range(H)], axis=0
        )
        for part in (slice(0, L // 2), slice(L // 2, L)):
            lg[part, :] = lax.dot_general(wt[part, :], held, NT, preferred_element_type=F32)
        tops, sums = [], []
        for to in range(Z):
            rows = slice(to * cb, (to + 1) * cb)
            part = lg[rows, :] + tbt[rows, 0:1]
            top = jnp.max(part, axis=0, keepdims=True)
            part = part - top
            for a in range(H):
                send[b, a, to] = part[:, a * iq : (a + 1) * iq].astype(BF16)
            bm[b, to] = top
            tops.append(top)
            sums.append(jnp.sum(jnp.exp(part), axis=0, keepdims=True))
        for i, a in enumerate((1 - h, h)):
            for k in z_order:
                to = ring(k)
                start_copy(send.at[b, a, to], rb.at[b, a, z], rb_sems.at[2 * group + i], at(nz=to))
        top = functools.reduce(jnp.maximum, tops)
        st[b, me] = top + jnp.log(sum(v * jnp.exp(t - top) for v, t in zip(sums, tops)))
        for ny, nx, nc in plane:
            start_copy(st.at[b, me], st.at[b, me], st_sems.at[group], at(ny=ny, nx=nx, nc=nc))

    def pair_head():
        wait_bytes(swr.at[pl.ds(0, Z - 1)], one.at[1])
        for j in range(Z // 2):
            turned = pltpu.roll(swr[j + Z // 2].astype(F32), lane_half, 1)
            swp[j] = (swr[j].astype(F32) + turned).astype(BF16)
        start_copy(swp, swq, one.at[0], at(nh=1 - h))

    for k in list(second) + near:
        arrived(k, x)
        if k in second:
            for px in row_out:
                forward(k, x, at(nx=px))
        to_core(k, x)
    for k in first:
        for px in row_in:
            arrived(k, px)
            to_core(k, px)
    pair_head()
    from_core(0)
    logits_of(0)
    for k in second:
        for px in row_in:
            arrived(k, px)
            to_core(k, px)
    for k in range(1, Z):
        block = ring(k) * C + c
        wait_bytes(sn.at[block], sn_sems.at[ring(k)])
        for e in other:
            start_copy(sn.at[block], sn.at[block], core_sems.at[2], at(nc=e))
    from_core(1)
    logits_of(1)

    if other:
        wait_bytes(sn.at[pl.ds(0, Z - 1)], core_sems.at[2])
    wait_bytes(swq, one.at[0])
    lane = lax.broadcasted_iota(jnp.int32, (cb, LANES), 1)
    theirs = jnp.where(lane >= lane_half, 1, 0) != h
    for j in range(Z // 2):
        packed = swq[j].astype(F32)
        turned = pltpu.roll(packed, lane_half, 1)
        for i, value in ((j, packed), (j + Z // 2, turned)):
            swx[i] = jnp.where(theirs, value, swr[i].astype(F32)).astype(BF16)
    scores = jnp.zeros((cb, ih), F32)
    for k in range(Z):
        part = slice(k * LANES, (k + 1) * LANES)
        scores = scores + lax.dot_general(
            swx[k], sn[:, :, part].reshape(ih, LANES), NT, preferred_element_type=F32
        )
    my_rows = pl.ds(pl.multiple_of(z * cb, 16), cb)
    alphas = jnp.exp(scores + sbt[my_rows, 0:1])
    al_s[...] = alphas
    ad[me] = jnp.sum(alphas, axis=0, keepdims=True)
    for a, b, e in plane:
        start_copy(ad.at[me], ad.at[me], one.at[2], at(ny=a, nx=b, nc=e))

    for group in range(2):
        b = column[groups[group][0]] // (Y // 2)
        wait_bytes(st.at[b, pl.ds(0, dpn - 1)], st_sems.at[group])
    tops = st[...]
    top = jnp.max(tops, axis=1)
    log_norm = top + jnp.log(jnp.sum(jnp.exp(tops - top[:, None]), axis=1))
    mine = z * H + h
    for b in range(2):
        shift = bm[b] - log_norm[b][None]
        for a in range(H):
            vs[:, a, b] = shift[:, :, a * iq : (a + 1) * iq]
    for k in z_order + [0]:
        start_copy(vs.at[ring(k), 1 - h], vr.at[mine], one.at[3], at(nz=ring(k), nh=1 - h))
    for k in z_order:
        start_copy(vs.at[ring(k), h], vr.at[mine], one.at[3], at(nz=ring(k)))
    vr[mine] = vs[z, h]

    halves = [column[group[0]] // (Y // 2) for group in groups]

    def summed(group, i):
        b, a = halves[group], (1 - h, h)[i]
        wait_bytes(rb.at[b, a, pl.ds(0, Z - 1)], rb_sems.at[2 * group + i])
        rb[b, a, z] = send[b, a, z]
        return b, jnp.sum(rb[b, a].astype(F32), axis=0)

    def to_partner(group):
        b, total = summed(group, 0)
        tb_s[b] = total.astype(BF16)
        start_copy(tb_s.at[b], tp.at[b], one.at[5], at(nh=1 - h))

    to_partner(0)
    wait_bytes(ad.at[pl.ds(0, dpn - 1)], one.at[2])
    asum[...] = jnp.sum(ad[...], axis=0)
    for k in z_order:
        start_copy(asum, az.at[z], one.at[4], at(nz=ring(k)))
    az[z] = asum[...]
    lgamma, digamma = gamma_parts(al_s[...])
    to_partner(1)
    for group in range(2):
        b, total = summed(group, 1)
        tz[b] = total
    wait_bytes(az.at[pl.ds(0, Z - 1)], one.at[4])
    lgamma_sum, digamma_sum = gamma_parts(jnp.sum(az[...], axis=0))
    wait_bytes(tp, one.at[5])
    wait_bytes(vr.at[pl.ds(0, Z * H - 1)], one.at[3])
    shift = jnp.sum(vr[...], axis=0)
    target = jnp.concatenate(
        [tz[b] + tp[b].astype(F32) + shift[b] for b in range(2)], axis=1
    ) / (Z * H)

    alphas = al_s[...]
    signal = alphas * (digamma - digamma_sum - target)
    terms = jnp.sum(lgamma - (alphas - 1.0) * target, axis=0, keepdims=True)
    terms = terms - lgamma_sum / (Z * dpn)
    deep = z * C + c
    ld[deep] = jnp.broadcast_to(jnp.sum(terms, axis=1, keepdims=True), (1, LANES))
    for k in z_order + [0]:
        for e in other + ([c] if k else []):
            start_copy(ld.at[deep], ld.at[deep], one.at[6], at(nz=ring(k), nc=e))

    high = signal.astype(BF16)
    rest = signal - high.astype(F32)
    mid = rest.astype(BF16)
    low = (rest - mid.astype(F32)).astype(BF16)
    parts = lax.dot_general(
        jnp.concatenate([high, mid, low], axis=0),
        sn[...].reshape(ih, D),
        (((1,), (0,)), ((), ())),
        preferred_element_type=F32,
    )
    grad = parts[:cb] + parts[cb : 2 * cb] + parts[2 * cb :]
    for k in range(Z):
        hs[k] = grad[:, k * LANES : (k + 1) * LANES].astype(BF16)
    for k in z_order:
        start_copy(hs.at[ring(k)], hr.at[z], one.at[7], at(nz=ring(k)))
    hr[z] = hs[z]
    bc[...] = jnp.zeros_like(bc)
    bc[my_rows, :] = jnp.broadcast_to(jnp.sum(signal, axis=1, keepdims=True), (cb, LANES))
    bg_s[...] = bc[...].T[0:1]
    for k in z_order:
        start_copy(bg_s, bgr.at[z], one.at[8], at(nz=ring(k)))
    bgr[z] = bg_s[...]

    wait_bytes(ld.at[pl.ds(0, Z * C - 1)], one.at[6])
    wide = (h * Y + y) * X + x
    lz[wide] = jnp.sum(ld[...], axis=0)
    for ph in (1 - h, h):
        for k in reversed(range(Y)):
            for px in row_out + ([x] if k or ph is not h else []):
                start_copy(lz.at[wide], lz.at[wide], one.at[9], at(nh=ph, ny=column[k], nx=px))

    wait_bytes(hr.at[pl.ds(0, Z - 1)], one.at[7])
    rows = hr[...].astype(F32).reshape(L, LANES).T
    ht[...] = rows.reshape(H, lane_half, L)
    hb[...] = ht[1 - h].astype(BF16)
    start_copy(hb, hp, one.at[10], at(nh=1 - h))
    wait_bytes(bgr.at[pl.ds(0, Z - 1)], one.at[8])
    bh[...] = jnp.sum(bgr[...], axis=0)
    start_copy(bh, bp, one.at[11], at(nh=1 - h))
    wait_bytes(hp, one.at[10])
    hg_o[...] = ht[h] + hp[...].astype(F32)
    wait_bytes(bp, one.at[11])
    bias_o[...] = ((bh[...] + bp[...]) / images).reshape(L)
    wait_bytes(lz.at[pl.ds(0, H * Y * X - 1)], one.at[9])
    loss_o[...] = jnp.sum(lz[...], axis=0) / (images * (L * dpn))

    wait_sum(sent, out)


def on_device(sizes, tf, tg, w, tb, sf, sg, sh, sb):
    Z, H, Y, X, C = sizes
    dpn = Y * X * C
    rows_t, D = tf.shape[1:]
    L = w.shape[2]
    cb = L // Z
    ih = rows_t * dpn // H
    iq = ih // 2
    rows_s = sf.shape[0]
    images = ih * H
    assert D == Z * LANES and rows_s * Z == ih and sh.shape[0] * H == LANES

    def v(shape, dtype=F32):
        return pltpu.VMEM(shape, dtype)

    scratch = [
        v((rows_t, D), BF16), v((1, D)), v((D, L), BF16), v((1, L)),
        v((rows_s, D), BF16), v((D,)), v((L,)), v((LANES // H, L), BF16),
        v((dpn, rows_t, D), BF16), v((L, D), BF16), v((L, LANES)), v((L, ih)),
        v((2, H, Z, cb, iq), BF16), v((2, H, Z, cb, iq), BF16), v((2, cb, iq)), v((2, cb, iq), BF16), v((2, cb, iq), BF16),
        v((2, Z, 1, ih)), v((2, dpn, 1, ih)), v((Z, H, 2, 1, iq)), v((Z * H, 2, 1, iq)),
        v((Z * C, rows_s // C, D), BF16), v((Z, cb, LANES), BF16), v((Z, cb, LANES), BF16),
        v((Z // 2, cb, LANES), BF16), v((Z // 2, cb, LANES), BF16), v((Z, cb, LANES), BF16),
        v((L, LANES)), v((dpn, 1, ih)), v((1, ih)), v((Z, 1, ih)), v((cb, ih)),
        v((L, LANES)), v((1, L)), v((Z, 1, L)), v((1, L)), v((1, L)),
        v((Z, cb, LANES), BF16), v((Z, cb, LANES), BF16), v((H, LANES // H, L)),
        v((LANES // H, L), BF16), v((LANES // H, L), BF16),
        v((Z * C, 1, LANES)), v((H * Y * X, 1, LANES)),
        v((2**15, LANES), BF16),
        pltpu.SemaphoreType.DMA((3,)), pltpu.SemaphoreType.DMA((Y * X,)), pltpu.SemaphoreType.DMA((3,)),
        pltpu.SemaphoreType.DMA((Z,)), pltpu.SemaphoreType.DMA((4,)), pltpu.SemaphoreType.DMA((2,)),
        pltpu.SemaphoreType.DMA((12,)), pltpu.SemaphoreType.DMA((1,)),
    ]
    vmem = pl.BlockSpec(memory_space=pltpu.VMEM)
    head_grad, bias_grad, loss = pl.pallas_call(
        functools.partial(step_kernel, sizes),
        out_shape=(
            jax.ShapeDtypeStruct((LANES // H, L), F32),
            jax.ShapeDtypeStruct((L,), F32),
            jax.ShapeDtypeStruct((1, LANES), F32),
        ),
        in_specs=[pl.BlockSpec(memory_space=pl.ANY)] * 8,
        out_specs=(vmem, vmem, vmem),
        scratch_shapes=scratch,
        compiler_params=pltpu.CompilerParams(
            collective_id=0, has_side_effects=True, vmem_limit_bytes=48 * 2**20
        ),
    )(*(pltpu.with_memory_space_constraint(a, pltpu.HBM) for a in (tf, tg, w, tb, sf, sg, sh, sb)))
    return loss[0, 0], head_grad / images, bias_grad


def solution(mesh, sizes=(8, 2, 4, 4, 2)):
    torus = Mesh(mesh.devices.reshape(sizes), AXES)
    placed = (
        P(MEMBER, DP, None),
        P(MEMBER, None),
        P(MEMBER, None, DP),
        P(MEMBER, DP),
        P(MEMBER, None),
        P(),
        P(MEMBER, DP),
        P(DP),
    )
    return jax.shard_map(
        functools.partial(on_device, sizes),
        mesh=torus,
        in_specs=placed,
        out_specs=(P(), P(MEMBER, DP), P(DP)),
        check_vma=False,
    )
```

time: 52.6 us -> 51.2 us (0.973)
  the two profiles are of different devices: /device:TPU:8 before, /device:TPU:1 now
where the time goes in v4:
time: 51.2 us; the launch traced here: 50.5 us
  Pallas kernels  47.4 us (93%)
  between operations  1.81 us (4%)
  other arithmetic  0.65 us (1%)
  local copies, waits for them, and re-layouts  0.58 us (1%)
    pallas_call x1, Pallas kernels, on_device(): pl.pallas_call(functools.partial(step_kernel, sizes), out_shape=(jax.Shap...  47.4 us

profile of v4, /device:TPU:1, one launch (start us, length us, event | category | flops | bytes accessed | tf_op | source)
XLA Modules:
  0.0 50.5 jit_solution(4563604606131119320)
XLA Ops:
  0.6 47.4 %shard_map.103 = (f32[64,384]{1,0:T(8,128)S(1)}, f32[384]{0:T(512)S(1)}, f32[1,128]{1,0:T(1,128)S(1)}) custom-call(bf16[1,16,1024]{2,1,0:T(8,128)(2,1)} %tf_h.1, f32[1,1024]{1,0:T(1,128)} %tg_h.1, bf16[1,1024,384]{2,1,0:T(8,128)(2,1)} %w_h.1, f32[1,384]{1,0:T(1,128)} %tb_h.1, bf16[32,1024]{1,0:T(8,128)(2,1)} %sf_h.1, f32[1024]{0:T(1024)} %sg_h.1, ...), custom_call_target="tpu_custom_call" | custom-call | tf_op jit(solution)/shard_map/pallas_call | solution.py:421
  48.1 0.6 %broadcast_multiply_fusion = f32[64,384]{1,0:T(8,128)} fusion(f32[64,384]{1,0:T(8,128)S(1)} %get-tuple-element.7), kind=kLoop, calls=%fused_computation | loop fusion | flops 24576 | bytes 196608 | tf_op jit(solution)/shard_map/div | solution.py:435
  48.7 0.6 %copy.14 = f32[384]{0:T(512)} copy(f32[384]{0:T(512)S(1)} %get-tuple-element.14) | data formatting | bytes 3072

commit v5 on v4

--- a/solution.py
+++ b/solution.py
@@ -55,11 +55,11 @@
     hg_o, bias_o, loss_o,
     tfv, tgv, wv, tbv, sfv, sgv, sbv, shv,
     xn, wt, tbt, lg, send, rb, tz, tb_s, tp,
-    bm, st, vs, vr,
+    bm, br, st, vs, vr,
     sn, sws, swr, swp, swq, swx, sbt, ad, asum, az, al_s,
     bc, bg_s, bgr, bh, bp, hs, hr, ht, hb, hp,
     ld, lz,
-    tally, in_sems, xn_sems, core_sems, sn_sems, rb_sems, st_sems, one, out_sems,
+    tally, in_sems, xn_sems, core_sems, sn_sems, rb_sems, st_sems, br_sems, one, out_sems,
 ):
     Z, H, Y, X, C = sizes
     z, h, y, x, c = (lax.axis_index(a) for a in AXES)
@@ -78,20 +78,38 @@
     images = ih * H
     lane_half = LANES // H
 
-    sent = []
-    out = out_sems.at[0]
-
-    def start_copy(src, dst, recv_sem, device):
-        sent.append(math.prod(src.shape) * src.dtype.itemsize)
+    hub = C - 1
+    sent = [[], [], []]
+
+    def start_copy(src, dst, recv_sem, device, kind=0):
+        sent[kind].append(math.prod(src.shape) * src.dtype.itemsize)
         pltpu.make_async_remote_copy(
             src_ref=src,
             dst_ref=dst,
-            send_sem=out,
+            send_sem=out_sems.at[kind],
             recv_sem=recv_sem,
             device_id=device,
             device_id_type=pl.DeviceIdType.MESH,
         ).start()
 
+    def to_own_hub(ref, recv_sem):
+        if C > 1:
+
+            @pl.when(c != hub)
+            def _():
+                start_copy(ref, ref, recv_sem, at(nc=hub), 2)
+
+    def wait_from_hubs(ref, count, sem):
+        @pl.when(c == hub)
+        def _():
+            wait_bytes(ref.at[pl.ds(0, count - 1)], sem)
+
+        if C > 1:
+
+            @pl.when(c != hub)
+            def _():
+                wait_bytes(ref.at[pl.ds(0, count)], sem)
+
     def wait_sum(sizes, sem):
         wait_bytes(tally.at[pl.ds(0, sum(sizes) // (2 * LANES))], sem)
 
@@ -109,11 +127,7 @@
 
     z_order = sorted(range(1, Z), key=lambda k: -min(k, Z - k))
     plane = [
-        (lax.rem(y + i, Y), lax.rem(x + j, X), lax.rem(c + k, C))
-        for i in reversed(range(Y))
-        for j in range(X)
-        for k in range(C)
-        if i or j or k
+        (lax.rem(y + i, Y), lax.rem(x + j, X)) for i in reversed(range(Y)) for j in range(X) if i or j
     ]
     column = [y]
     if Y > 1:
@@ -122,10 +136,12 @@
         column.append((column[k - 2] + 2) % Y)
     groups = [range(0, Y // 2), range(Y // 2, Y)]
     first, second = groups
+    halves = [column[group[0]] // (Y // 2) for group in groups]
     near = [k for k in first if k]
     row_out = [lax.rem(x + j, X) for j in (2, 1, 3) if j < X]
     row_in = [lax.rem(x + j, X) for j in (1, 3, 2) if j < X]
     other = [lax.rem(c + e, C) for e in range(1, C)]
+    twin = (other + [c])[0]
 
     loads = []
     for i, group in enumerate(
@@ -139,9 +155,11 @@
             pltpu.make_async_copy(src, dst, in_sems.at[i]).start()
         loads.append([math.prod(dst.shape) * dst.dtype.itemsize for _, dst in group])
     barrier = pltpu.get_barrier_semaphore()
-    peers = [at(ny=column[k]) for k in range(1, Y)] + [at(nx=px) for px in row_out]
-    peers += [at(ny=column[k], nx=px) for k in near for px in row_out]
+    peers = [at(ny=column[k], nc=twin) for k in range(1, Y)]
+    peers += [at(nx=px, nc=twin) for px in row_out]
+    peers += [at(ny=column[k], nx=px, nc=twin) for k in near for px in row_out]
     peers += [at(nc=e) for e in other] + [at(nz=ring(k)) for k in range(1, Z)] + [at(nh=1 - h)]
+    peers += [at(nz=ring(k), nc=e) for k in range(1, Z) for e in other]
     for peer in peers:
         pl.semaphore_signal(barrier, 1, device_id=peer, device_id_type=pl.DeviceIdType.MESH)
 
@@ -150,23 +168,28 @@
     xn[own] = norm_rows(tfv[...], tgv[...]).astype(BF16)
     pl.semaphore_wait(barrier, len(peers))
 
+    def origin(k, px):
+        if k == 0 and px is x:
+            return c
+        return c if k in second and px is not x else twin
+
     def forward(k, px, device):
-        block = spot(column[k], px, c)
+        block = spot(column[k], px, origin(k, px))
         start_copy(xn.at[block], xn.at[block], xn_sems.at[column[k] * X + px], device)
 
     def arrived(k, px):
-        wait_bytes(xn.at[spot(column[k], px, c)], xn_sems.at[column[k] * X + px])
+        wait_bytes(xn.at[spot(column[k], px, origin(k, px))], xn_sems.at[column[k] * X + px])
 
     def to_core(k, px):
-        block = spot(column[k], px, c)
+        block = spot(column[k], px, origin(k, px))
         for e in other:
             start_copy(xn.at[block], xn.at[block], core_sems.at[int(k in second)], at(nc=e))
 
     for k in list(second) + near:
-        forward(0, x, at(ny=column[k]))
+        forward(0, x, at(ny=column[k], nc=twin))
     for k in [0] + near:
         for px in row_out:
-            forward(0, x, at(ny=column[k], nx=px))
+            forward(0, x, at(ny=column[k], nx=px, nc=twin))
     to_core(0, x)
     wait_sum(loads[1], in_sems.at[1])
     head = shv[...].astype(F32)
@@ -180,7 +203,7 @@
     sn[pl.ds(z * C, C)] = normed_s.reshape(C, rows_s // C, D)
     mine = z * C + c
     for k in z_order:
-        start_copy(sn.at[mine], sn.at[mine], sn_sems.at[z], at(nz=ring(k)))
+        start_copy(sn.at[mine], sn.at[mine], sn_sems.at[z], at(nz=ring(k), nc=twin))
 
     wait_sum(loads[2], in_sems.at[2])
     tbt[...] = jnp.broadcast_to(tbv[...], (LANES, L)).T
@@ -194,7 +217,7 @@
             wait_bytes(xn.at[pl.ds(0, len(groups[group]) * X)], core_sems.at[group])
 
     def logits_of(group):
-        b = column[groups[group][0]] // (Y // 2)
+        b = halves[group]
         held = jnp.concatenate(
             [xn[pl.ds(a * half_blocks + b * qb, qb)].reshape(iq, D) for a in range(H)], axis=0
         )
@@ -208,7 +231,8 @@
             part = part - top
             for a in range(H):
                 send[b, a, to] = part[:, a * iq : (a + 1) * iq].astype(BF16)
-            bm[b, to] = top
+            for a in range(H):
+                bm[to, a, b] = top[:, a * iq : (a + 1) * iq]
             tops.append(top)
             sums.append(jnp.sum(jnp.exp(part), axis=0, keepdims=True))
         for i, a in enumerate((1 - h, h)):
@@ -217,8 +241,9 @@
                 start_copy(send.at[b, a, to], rb.at[b, a, z], rb_sems.at[2 * group + i], at(nz=to))
         top = functools.reduce(jnp.maximum, tops)
         st[b, me] = top + jnp.log(sum(v * jnp.exp(t - top) for v, t in zip(sums, tops)))
-        for ny, nx, nc in plane:
-            start_copy(st.at[b, me], st.at[b, me], st_sems.at[group], at(ny=ny, nx=nx, nc=nc))
+        for ny, nx in plane:
+            start_copy(st.at[b, me], st.at[b, me], st_sems.at[group], at(ny=ny, nx=nx, nc=hub))
+        to_own_hub(st.at[b, me], st_sems.at[group])
 
     def pair_head():
         wait_bytes(swr.at[pl.ds(0, Z - 1)], one.at[1])
@@ -231,7 +256,7 @@
         arrived(k, x)
         if k in second:
             for px in row_out:
-                forward(k, x, at(nx=px))
+                forward(k, x, at(nx=px, nc=twin))
         to_core(k, x)
     for k in first:
         for px in row_in:
@@ -244,14 +269,20 @@
         for px in row_in:
             arrived(k, px)
             to_core(k, px)
+    from_core(1)
+    logits_of(1)
+    member = z * H + h
+    for k in z_order + [0]:
+        for ph in (1 - h, h):
+            if k or ph is not h:
+                start_copy(bm.at[ring(k), ph], br.at[member], br_sems.at[0], at(nz=ring(k), nh=ph))
+    br[member] = bm[z, h]
+
     for k in range(1, Z):
-        block = ring(k) * C + c
+        block = ring(k) * C + twin
         wait_bytes(sn.at[block], sn_sems.at[ring(k)])
         for e in other:
             start_copy(sn.at[block], sn.at[block], core_sems.at[2], at(nc=e))
-    from_core(1)
-    logits_of(1)
-
     if other:
         wait_bytes(sn.at[pl.ds(0, Z - 1)], core_sems.at[2])
     wait_bytes(swq, one.at[0])
@@ -272,27 +303,27 @@
     alphas = jnp.exp(scores + sbt[my_rows, 0:1])
     al_s[...] = alphas
     ad[me] = jnp.sum(alphas, axis=0, keepdims=True)
-    for a, b, e in plane:
-        start_copy(ad.at[me], ad.at[me], one.at[2], at(ny=a, nx=b, nc=e))
-
-    for group in range(2):
-        b = column[groups[group][0]] // (Y // 2)
-        wait_bytes(st.at[b, pl.ds(0, dpn - 1)], st_sems.at[group])
-    tops = st[...]
-    top = jnp.max(tops, axis=1)
-    log_norm = top + jnp.log(jnp.sum(jnp.exp(tops - top[:, None]), axis=1))
-    mine = z * H + h
-    for b in range(2):
-        shift = bm[b] - log_norm[b][None]
+    for ny, nx in plane:
+        start_copy(ad.at[me], ad.at[me], one.at[2], at(ny=ny, nx=nx, nc=hub))
+    to_own_hub(ad.at[me], one.at[2])
+
+    @pl.when(c == hub)
+    def _():
+        for group in range(2):
+            wait_bytes(st.at[halves[group], pl.ds(0, dpn - 1)], st_sems.at[group])
+        tops = st[...]
+        top = jnp.max(tops, axis=1)
+        log_norm = top + jnp.log(jnp.sum(jnp.exp(tops - top[:, None]), axis=1))
         for a in range(H):
-            vs[:, a, b] = shift[:, :, a * iq : (a + 1) * iq]
-    for k in z_order + [0]:
-        start_copy(vs.at[ring(k), 1 - h], vr.at[mine], one.at[3], at(nz=ring(k), nh=1 - h))
-    for k in z_order:
-        start_copy(vs.at[ring(k), h], vr.at[mine], one.at[3], at(nz=ring(k)))
-    vr[mine] = vs[z, h]
-
-    halves = [column[group[0]] // (Y // 2) for group in groups]
+            vs[a] = log_norm[:, :, a * iq : (a + 1) * iq]
+        for k in z_order + [0]:
+            for ph in (1 - h, h):
+                for e in other + [c]:
+                    if k or ph is not h or e is not c:
+                        start_copy(
+                            vs.at[ph], vr.at[member], one.at[3], at(nz=ring(k), nh=ph, nc=e), 1
+                        )
+        vr[member] = vs[h]
 
     def summed(group, i):
         b, a = halves[group], (1 - h, h)[i]
@@ -306,35 +337,34 @@
         start_copy(tb_s.at[b], tp.at[b], one.at[5], at(nh=1 - h))
 
     to_partner(0)
-    wait_bytes(ad.at[pl.ds(0, dpn - 1)], one.at[2])
-    asum[...] = jnp.sum(ad[...], axis=0)
-    for k in z_order:
-        start_copy(asum, az.at[z], one.at[4], at(nz=ring(k)))
-    az[z] = asum[...]
+    @pl.when(c == hub)
+    def _():
+        wait_bytes(ad.at[pl.ds(0, dpn - 1)], one.at[2])
+        asum[...] = jnp.sum(ad[...], axis=0)
+        for k in z_order + [0]:
+            for e in other + [c]:
+                if k or e is not c:
+                    start_copy(asum, az.at[z], one.at[4], at(nz=ring(k), nc=e), 1)
+        az[z] = asum[...]
+
     lgamma, digamma = gamma_parts(al_s[...])
     to_partner(1)
     for group in range(2):
         b, total = summed(group, 1)
         tz[b] = total
-    wait_bytes(az.at[pl.ds(0, Z - 1)], one.at[4])
+    wait_from_hubs(az, Z, one.at[4])
     lgamma_sum, digamma_sum = gamma_parts(jnp.sum(az[...], axis=0))
     wait_bytes(tp, one.at[5])
-    wait_bytes(vr.at[pl.ds(0, Z * H - 1)], one.at[3])
-    shift = jnp.sum(vr[...], axis=0)
+    wait_bytes(br.at[pl.ds(0, Z * H - 1)], br_sems.at[0])
+    shift = jnp.sum(br[...], axis=0)
+    wait_from_hubs(vr, Z * H, one.at[3])
+    shift = shift - jnp.sum(vr[...], axis=0)
     target = jnp.concatenate(
         [tz[b] + tp[b].astype(F32) + shift[b] for b in range(2)], axis=1
     ) / (Z * H)
 
     alphas = al_s[...]
     signal = alphas * (digamma - digamma_sum - target)
-    terms = jnp.sum(lgamma - (alphas - 1.0) * target, axis=0, keepdims=True)
-    terms = terms - lgamma_sum / (Z * dpn)
-    deep = z * C + c
-    ld[deep] = jnp.broadcast_to(jnp.sum(terms, axis=1, keepdims=True), (1, LANES))
-    for k in z_order + [0]:
-        for e in other + ([c] if k else []):
-            start_copy(ld.at[deep], ld.at[deep], one.at[6], at(nz=ring(k), nc=e))
-
     high = signal.astype(BF16)
     rest = signal - high.astype(F32)
     mid = rest.astype(BF16)
@@ -351,6 +381,15 @@
     for k in z_order:
         start_copy(hs.at[ring(k)], hr.at[z], one.at[7], at(nz=ring(k)))
     hr[z] = hs[z]
+
+    terms = jnp.sum(lgamma - (alphas - 1.0) * target, axis=0, keepdims=True)
+    terms = terms - lgamma_sum / (Z * dpn)
+    deep = z * C + c
+    ld[deep] = jnp.broadcast_to(jnp.sum(terms, axis=1, keepdims=True), (1, LANES))
+    for k in z_order:
+        start_copy(ld.at[deep], ld.at[deep], one.at[6], at(nz=ring(k), nc=hub))
+    to_own_hub(ld.at[deep], one.at[6])
+
     bc[...] = jnp.zeros_like(bc)
     bc[my_rows, :] = jnp.broadcast_to(jnp.sum(signal, axis=1, keepdims=True), (cb, LANES))
     bg_s[...] = bc[...].T[0:1]
@@ -358,13 +397,23 @@
         start_copy(bg_s, bgr.at[z], one.at[8], at(nz=ring(k)))
     bgr[z] = bg_s[...]
 
-    wait_bytes(ld.at[pl.ds(0, Z * C - 1)], one.at[6])
-    wide = (h * Y + y) * X + x
-    lz[wide] = jnp.sum(ld[...], axis=0)
-    for ph in (1 - h, h):
-        for k in reversed(range(Y)):
-            for px in row_out + ([x] if k or ph is not h else []):
-                start_copy(lz.at[wide], lz.at[wide], one.at[9], at(nh=ph, ny=column[k], nx=px))
+    @pl.when(c == hub)
+    def _():
+        wait_bytes(ld.at[pl.ds(0, Z * C - 1)], one.at[6])
+        wide = (h * Y + y) * X + x
+        lz[wide] = jnp.sum(ld[...], axis=0)
+        for ph in (1 - h, h):
+            for k in reversed(range(Y)):
+                for px in row_out + [x]:
+                    for e in other + [c]:
+                        if k or ph is not h or px is not x or e is not c:
+                            start_copy(
+                                lz.at[wide],
+                                lz.at[wide],
+                                one.at[9],
+                                at(nh=ph, ny=column[k], nx=px, nc=e),
+                                1,
+                            )
 
     wait_bytes(hr.at[pl.ds(0, Z - 1)], one.at[7])
     rows = hr[...].astype(F32).reshape(L, LANES).T
@@ -375,13 +424,34 @@
     bh[...] = jnp.sum(bgr[...], axis=0)
     start_copy(bh, bp, one.at[11], at(nh=1 - h))
     wait_bytes(hp, one.at[10])
-    hg_o[...] = ht[h] + hp[...].astype(F32)
+    hg_o[...] = (ht[h] + hp[...].astype(F32)) / images
     wait_bytes(bp, one.at[11])
     bias_o[...] = ((bh[...] + bp[...]) / images).reshape(L)
-    wait_bytes(lz.at[pl.ds(0, H * Y * X - 1)], one.at[9])
+    wait_from_hubs(lz, H * Y * X, one.at[9])
     loss_o[...] = jnp.sum(lz[...], axis=0) / (images * (L * dpn))
 
-    wait_sum(sent, out)
+    wait_sum(sent[0], out_sems.at[0])
+
+    @pl.when(c == hub)
+    def _():
+        wait_sum(sent[1], out_sems.at[1])
+
+    if C > 1:
+
+        @pl.when(c != hub)
+        def _():
+            wait_sum(sent[2], out_sems.at[2])
+
+
+def deliver(hg, bias, loss, hg_o, bias_o, loss_o, sems):
+    copies = [
+        pltpu.make_async_copy(src, dst, sems.at[i])
+        for i, (src, dst) in enumerate([(hg, hg_o), (bias, bias_o), (loss, loss_o)])
+    ]
+    for copy in copies:
+        copy.start()
+    for copy in copies:
+        copy.wait()
 
 
 def on_device(sizes, tf, tg, w, tb, sf, sg, sh, sb):
@@ -404,7 +474,7 @@
         v((rows_s, D), BF16), v((D,)), v((L,)), v((LANES // H, L), BF16),
         v((dpn, rows_t, D), BF16), v((L, D), BF16), v((L, LANES)), v((L, ih)),
         v((2, H, Z, cb, iq), BF16), v((2, H, Z, cb, iq), BF16), v((2, cb, iq)), v((2, cb, iq), BF16), v((2, cb, iq), BF16),
-        v((2, Z, 1, ih)), v((2, dpn, 1, ih)), v((Z, H, 2, 1, iq)), v((Z * H, 2, 1, iq)),
+        v((Z, H, 2, 1, iq)), v((Z * H, 2, 1, iq)), v((2, dpn, 1, ih)), v((H, 2, 1, iq)), v((Z * H, 2, 1, iq)),
         v((Z * C, rows_s // C, D), BF16), v((Z, cb, LANES), BF16), v((Z, cb, LANES), BF16),
         v((Z // 2, cb, LANES), BF16), v((Z // 2, cb, LANES), BF16), v((Z, cb, LANES), BF16),
         v((L, LANES)), v((dpn, 1, ih)), v((1, ih)), v((Z, 1, ih)), v((cb, ih)),
@@ -414,8 +484,8 @@
         v((Z * C, 1, LANES)), v((H * Y * X, 1, LANES)),
         v((2**15, LANES), BF16),
         pltpu.SemaphoreType.DMA((3,)), pltpu.SemaphoreType.DMA((Y * X,)), pltpu.SemaphoreType.DMA((3,)),
-        pltpu.SemaphoreType.DMA((Z,)), pltpu.SemaphoreType.DMA((4,)), pltpu.SemaphoreType.DMA((2,)),
-        pltpu.SemaphoreType.DMA((12,)), pltpu.SemaphoreType.DMA((1,)),
+        pltpu.SemaphoreType.DMA((Z,)), pltpu.SemaphoreType.DMA((4,)), pltpu.SemaphoreType.DMA((2,)), pltpu.SemaphoreType.DMA((1,)),
+        pltpu.SemaphoreType.DMA((12,)), pltpu.SemaphoreType.DMA((3,)),
     ]
     vmem = pl.BlockSpec(memory_space=pltpu.VMEM)
     head_grad, bias_grad, loss = pl.pallas_call(
@@ -432,7 +502,19 @@
             collective_id=0, has_side_effects=True, vmem_limit_bytes=48 * 2**20
         ),
     )(*(pltpu.with_memory_space_constraint(a, pltpu.HBM) for a in (tf, tg, w, tb, sf, sg, sh, sb)))
-    return loss[0, 0], head_grad / images, bias_grad
+    head_grad, bias_grad, loss = pl.pallas_call(
+        deliver,
+        out_shape=(
+            jax.ShapeDtypeStruct((LANES // H, L), F32),
+            jax.ShapeDtypeStruct((L,), F32),
+            jax.ShapeDtypeStruct((1, LANES), F32),
+        ),
+        in_specs=[vmem] * 3,
+        out_specs=[pl.BlockSpec(memory_space=pl.ANY)] * 3,
+        scratch_shapes=[pltpu.SemaphoreType.DMA((3,))],
+        compiler_params=pltpu.CompilerParams(vmem_limit_bytes=2**20),
+    )(head_grad, bias_grad, loss)
+    return loss[0, 0], head_grad, bias_grad
 
 
 def solution(mesh, sizes=(8, 2, 4, 4, 2)):

time: 51.2 us -> 50.1 us (0.979); the launches traced: 50.5 us -> 50 us
  Pallas kernels: 47.4 us -> 49.3 us
  between operations: 1.81 us -> 0.64 us
  other arithmetic: 0.65 us -> 0 us
  local copies, waits for them, and re-layouts: 0.58 us -> 0 us
    pallas_call x1, Pallas kernels: 47.4 us -> 48.7 us  [on_device(): pl.pallas_call(functools.partial(step_kernel, sizes), out_shape=(jax.Shap...]
    pallas_call x0 -> x1, Pallas kernels: none -> 0.67 us  [on_device(): pl.pallas_call(deliver, out_shape=(jax.ShapeDtypeStruct((LANES // H, L),...]
    div x1 -> x0, other arithmetic: 0.65 us -> none  [on_device(): return (loss[0, 0], head_grad / images, bias_grad)]
    unnamed x1 -> x0, local copies, waits for them, and re-layouts: 0.58 us -> none
where the time goes in v5:
time: 50.1 us; the launch traced here: 50 us
  Pallas kernels  49.3 us (98%)
  between operations  0.64 us (1%)
    pallas_call x1, Pallas kernels, on_device(): pl.pallas_call(functools.partial(step_kernel, sizes), out_shape=(jax.Shap...  48.7 us

profile of v5, /device:TPU:1, one launch (start us, length us, event | category | flops | bytes accessed | tf_op | source)
XLA Modules:
  0.0 50.0 jit_solution(10784722701234164266)
XLA Ops:
  0.6 48.7 %shard_map.103 = (f32[64,384]{1,0:T(8,128)S(1)}, f32[384]{0:T(512)S(1)}, f32[1,128]{1,0:T(1,128)S(1)}) custom-call(bf16[1,16,1024]{2,1,0:T(8,128)(2,1)} %tf_h.1, f32[1,1024]{1,0:T(1,128)} %tg_h.1, bf16[1,1024,384]{2,1,0:T(8,128)(2,1)} %w_h.1, f32[1,384]{1,0:T(1,128)} %tb_h.1, bf16[32,1024]{1,0:T(8,128)(2,1)} %sf_h.1, f32[1024]{0:T(1024)} %sg_h.1, ...), custom_call_target="tpu_custom_call" | custom-call | tf_op jit(solution)/shard_map/pallas_call | solution.py:491
  49.3 0.7 %shard_map.104 = (f32[64,384]{1,0:T(8,128)}, f32[384]{0:T(512)}, f32[1,128]{1,0:T(1,128)}) custom-call(f32[64,384]{1,0:T(8,128)S(1)} %get-tuple-element.9.hg, f32[384]{0:T(512)S(1)} %get-tuple-element.10.bias, f32[1,128]{1,0:T(1,128)S(1)} %get-tuple-element.11.loss), custom_call_target="tpu_custom_call" | custom-call | tf_op jit(solution)/shard_map/pallas_call | solution.py:505

commit v6 on v5

--- a/solution.py
+++ b/solution.py
@@ -59,7 +59,7 @@
     sn, sws, swr, swp, swq, swx, sbt, ad, asum, az, al_s,
     bc, bg_s, bgr, bh, bp, hs, hr, ht, hb, hp,
     ld, lz,
-    tally, in_sems, xn_sems, core_sems, sn_sems, rb_sems, st_sems, br_sems, one, out_sems,
+    tally, in_sems, xn_sems, core_sems, rb_sems, st_sems, br_sems, one, out_sems,
 ):
     Z, H, Y, X, C = sizes
     z, h, y, x, c = (lax.axis_index(a) for a in AXES)
@@ -141,7 +141,6 @@
     row_out = [lax.rem(x + j, X) for j in (2, 1, 3) if j < X]
     row_in = [lax.rem(x + j, X) for j in (1, 3, 2) if j < X]
     other = [lax.rem(c + e, C) for e in range(1, C)]
-    twin = (other + [c])[0]
 
     loads = []
     for i, group in enumerate(
@@ -155,11 +154,9 @@
             pltpu.make_async_copy(src, dst, in_sems.at[i]).start()
         loads.append([math.prod(dst.shape) * dst.dtype.itemsize for _, dst in group])
     barrier = pltpu.get_barrier_semaphore()
-    peers = [at(ny=column[k], nc=twin) for k in range(1, Y)]
-    peers += [at(nx=px, nc=twin) for px in row_out]
-    peers += [at(ny=column[k], nx=px, nc=twin) for k in near for px in row_out]
+    peers = [at(ny=column[k]) for k in range(1, Y)] + [at(nx=px) for px in row_out]
+    peers += [at(ny=column[k], nx=px) for k in near for px in row_out]
     peers += [at(nc=e) for e in other] + [at(nz=ring(k)) for k in range(1, Z)] + [at(nh=1 - h)]
-    peers += [at(nz=ring(k), nc=e) for k in range(1, Z) for e in other]
     for peer in peers:
         pl.semaphore_signal(barrier, 1, device_id=peer, device_id_type=pl.DeviceIdType.MESH)
 
@@ -168,28 +165,23 @@
     xn[own] = norm_rows(tfv[...], tgv[...]).astype(BF16)
     pl.semaphore_wait(barrier, len(peers))
 
-    def origin(k, px):
-        if k == 0 and px is x:
-            return c
-        return c if k in second and px is not x else twin
-
     def forward(k, px, device):
-        block = spot(column[k], px, origin(k, px))
+        block = spot(column[k], px, c)
         start_copy(xn.at[block], xn.at[block], xn_sems.at[column[k] * X + px], device)
 
     def arrived(k, px):
-        wait_bytes(xn.at[spot(column[k], px, origin(k, px))], xn_sems.at[column[k] * X + px])
+        wait_bytes(xn.at[spot(column[k], px, c)], xn_sems.at[column[k] * X + px])
 
     def to_core(k, px):
-        block = spot(column[k], px, origin(k, px))
+        block = spot(column[k], px, c)
         for e in other:
             start_copy(xn.at[block], xn.at[block], core_sems.at[int(k in second)], at(nc=e))
 
     for k in list(second) + near:
-        forward(0, x, at(ny=column[k], nc=twin))
+        forward(0, x, at(ny=column[k]))
     for k in [0] + near:
         for px in row_out:
-            forward(0, x, at(ny=column[k], nx=px, nc=twin))
+            forward(0, x, at(ny=column[k], nx=px))
     to_core(0, x)
     wait_sum(loads[1], in_sems.at[1])
     head = shv[...].astype(F32)
@@ -203,7 +195,7 @@
     sn[pl.ds(z * C, C)] = normed_s.reshape(C, rows_s // C, D)
     mine = z * C + c
     for k in z_order:
-        start_copy(sn.at[mine], sn.at[mine], sn_sems.at[z], at(nz=ring(k), nc=twin))
+        start_copy(sn.at[mine], sn.at[mine], core_sems.at[3], at(nz=ring(k)))
 
     wait_sum(loads[2], in_sems.at[2])
     tbt[...] = jnp.broadcast_to(tbv[...], (LANES, L)).T
@@ -256,7 +248,7 @@
         arrived(k, x)
         if k in second:
             for px in row_out:
-                forward(k, x, at(nx=px, nc=twin))
+                forward(k, x, at(nx=px))
         to_core(k, x)
     for k in first:
         for px in row_in:
@@ -278,9 +270,9 @@
                 start_copy(bm.at[ring(k), ph], br.at[member], br_sems.at[0], at(nz=ring(k), nh=ph))
     br[member] = bm[z, h]
 
+    wait_bytes(sn.at[pl.ds(0, Z - 1)], core_sems.at[3])
     for k in range(1, Z):
-        block = ring(k) * C + twin
-        wait_bytes(sn.at[block], sn_sems.at[ring(k)])
+        block = ring(k) * C + c
         for e in other:
             start_copy(sn.at[block], sn.at[block], core_sems.at[2], at(nc=e))
     if other:
@@ -483,8 +475,8 @@
         v((LANES // H, L), BF16), v((LANES // H, L), BF16),
         v((Z * C, 1, LANES)), v((H * Y * X, 1, LANES)),
         v((2**15, LANES), BF16),
-        pltpu.SemaphoreType.DMA((3,)), pltpu.SemaphoreType.DMA((Y * X,)), pltpu.SemaphoreType.DMA((3,)),
-        pltpu.SemaphoreType.DMA((Z,)), pltpu.SemaphoreType.DMA((4,)), pltpu.SemaphoreType.DMA((2,)), pltpu.SemaphoreType.DMA((1,)),
+        pltpu.SemaphoreType.DMA((3,)), pltpu.SemaphoreType.DMA((Y * X,)), pltpu.SemaphoreType.DMA((4,)),
+        pltpu.SemaphoreType.DMA((4,)), pltpu.SemaphoreType.DMA((2,)), pltpu.SemaphoreType.DMA((1,)),
         pltpu.SemaphoreType.DMA((12,)), pltpu.SemaphoreType.DMA((3,)),
     ]
     vmem = pl.BlockSpec(memory_space=pltpu.VMEM)

time: 50.1 us -> 49.8 us (level)
  no operation moved by 1% of the time
where the time goes in v6:
time: 49.8 us; the launch traced here: 49.7 us
  Pallas kernels  49 us (98%)
  between operations  0.64 us (1%)
    pallas_call x1, Pallas kernels, on_device(): pl.pallas_call(functools.partial(step_kernel, sizes), out_shape=(jax.Shap...  48.4 us

profile of v6, /device:TPU:1, one launch (start us, length us, event | category | flops | bytes accessed | tf_op | source)
XLA Modules:
  0.0 49.7 jit_solution(18078314501780382826)
XLA Ops:
  0.6 48.4 %shard_map.103 = (f32[64,384]{1,0:T(8,128)S(1)}, f32[384]{0:T(512)S(1)}, f32[1,128]{1,0:T(1,128)S(1)}) custom-call(bf16[1,16,1024]{2,1,0:T(8,128)(2,1)} %tf_h.1, f32[1,1024]{1,0:T(1,128)} %tg_h.1, bf16[1,1024,384]{2,1,0:T(8,128)(2,1)} %w_h.1, f32[1,384]{1,0:T(1,128)} %tb_h.1, bf16[32,1024]{1,0:T(8,128)(2,1)} %sf_h.1, f32[1024]{0:T(1024)} %sg_h.1, ...), custom_call_target="tpu_custom_call" | custom-call | tf_op jit(solution)/shard_map/pallas_call | solution.py:483
  49.0 0.7 %shard_map.104 = (f32[64,384]{1,0:T(8,128)}, f32[384]{0:T(512)}, f32[1,128]{1,0:T(1,128)}) custom-call(f32[64,384]{1,0:T(8,128)S(1)} %get-tuple-element.9.hg, f32[384]{0:T(512)S(1)} %get-tuple-element.10.bias, f32[1,128]{1,0:T(1,128)S(1)} %get-tuple-element.11.loss), custom_call_target="tpu_custom_call" | custom-call | tf_op jit(solution)/shard_map/pallas_call | solution.py:497
